TPU v7x, 128 devices: a whole 4x4x4 slice. The times are simulated.
128 devices in a mesh: rows: 16 (over y, x), dict: 8 (over z, core).
Axes of the slice: x: 4, y: 4, z: 4, core: 2. Of those that a mesh axis runs over, the one named last changes fastest.
Arguments:
- lookup_keys_per_record: int32 [524288], P(('rows', 'dict')), may hold values from 0 to 65535, as said below
- filter_passed_flags: int32 [524288], P(('rows', 'dict')), may hold values from 0 to 1
- decoding_table: bfloat16 [65536, 128], P('dict'), may hold values from -6 to 6
Outputs:
- compacted: bfloat16 [524288, 128], P(('rows', 'dict'))
Inputs may be any that keep to these rules, and one draw needn't show every extreme that they name: Codes of the rows of one device lie in one range of 8192 consecutive lookup_keys_per_record (k * 8192 to (k + 1) * 8192 - 1) at most 1024 times, and exactly 1024 times for some range, whose rows all survive.
All inputs are finite; a program needn't handle non-finite values.
Results may differ from a plain program's by a relative error of at most 0.001.
Values may be sent and summed in bfloat16 or wider, within the bound.
No kernel may reach another device: no remote copies, remote signals or barrier semaphores. Data moves between devices by JAX's collectives and lax.ppermute only.
A program may use at most 64 MiB of HBM per device.

v0:
```python
import jax
import jax.numpy as jnp
from jax import lax
from jax.sharding import PartitionSpec as P


def sent_to_all(shard, axis):
    size = lax.axis_size(axis)
    return lax.all_to_all(
        jnp.broadcast_to(shard[None], (size, *shard.shape)), axis, 0, 0, tiled=True
    )


def folded_in_pairs(pieces, combine):
    while len(jax.tree.leaves(pieces)[0]) > 1:
        pieces = jax.vmap(combine)(*(pieces[side::2] for side in (0, 1)))
    return pieces[0]


def carried_in(shard, axis, combine, identity):
    size, mine = (lax.axis_size(axis), lax.axis_index(axis))
    passed = jnp.arange(size) < mine

    def kept(part, zero, own):
        part = jnp.where(
            passed.reshape(-1, *(1 for _ in own.shape)), part, jnp.asarray(zero, own.dtype)
        )
        return part

    pieces = sent_to_all(shard, axis)
    return folded_in_pairs(kept(pieces, identity, shard), combine)


def from_behind(shard, axis, by):
    size = lax.axis_size(axis)
    pairs = [(i, i + by) for i in range(size) if 0 <= i + by < size]
    return lax.ppermute(shard, axis, pairs)


def summed_tallies(earlier, later):
    return earlier + later


def on_device(lookup_keys_per_record, filter_passed_flags, decoding_table):
    rows_here = lookup_keys_per_record.shape[0]
    devices = lax.axis_size("rows") * lax.axis_size("dict")
    keeper_flags = filter_passed_flags > 0
    kept_tally = jnp.sum(filter_passed_flags)
    before_group = carried_in(kept_tally, "dict", summed_tallies, jnp.int32(0))
    group_sum = lax.psum(kept_tally, "dict")
    before_rows = carried_in(group_sum, "rows", summed_tallies, jnp.int32(0))
    beginning_offset = before_group + before_rows
    shard_inner_position = jnp.cumsum(filter_passed_flags) - 1
    whole = lax.all_gather(decoding_table, "dict", axis=0, tiled=True)
    picked = jnp.take(whole, lookup_keys_per_record, axis=0)
    values = jnp.where(keeper_flags[:, None], picked, jnp.zeros_like(picked))
    device_index = lax.axis_index(("rows", "dict"))
    position = jnp.arange(rows_here, dtype=jnp.int32)
    distance = device_index * rows_here - beginning_offset + position - shard_inner_position
    tagged = jnp.where(keeper_flags, distance + 1, 0).astype(jnp.int32)
    total_bits = (devices * rows_here - 1).bit_length()
    for level in range(total_bits):
        step = 1 << level
        whole_hops, rest = divmod(step, rows_here)
        present = tagged > 0
        moving = present & (tagged - 1 >> level & 1 == 1)
        staying = present & jnp.logical_not(moving)
        send_values = jnp.where(moving[:, None], values, jnp.zeros_like(values))
        send_tags = jnp.where(moving, tagged, 0)
        if whole_hops > 0:
            far_values, far_tags = from_behind(
                (send_values, send_tags), ("rows", "dict"), -whole_hops
            )
        else:
            far_values, far_tags = (send_values, send_tags)
        if rest > 0:
            head_values, head_tags = from_behind(
                (send_values[:rest], send_tags[:rest]), ("rows", "dict"), -(whole_hops + 1)
            )
            arrived_values = jnp.concatenate([far_values[rest:], head_values], axis=0)
            arrived_tags = jnp.concatenate([far_tags[rest:], head_tags], axis=0)
        else:
            arrived_values, arrived_tags = (far_values, far_tags)
        values = jnp.where(staying[:, None], values, arrived_values)
        tagged = jnp.where(staying, tagged, arrived_tags)
    return values


def solution(mesh):
    placed = (P(("rows", "dict")), P(("rows", "dict")), P("dict", None))
    return jax.shard_map(
        on_device, mesh=mesh, in_specs=placed, out_specs=P(("rows", "dict"), None), check_vma=False
    )
```

profile of v0, /device:TPU:4, one launch (start us, length us, event | category | flops | bytes accessed | tf_op | source)
XLA Modules:
  0.0 502.0 jit_solution(14463343271263238570)
XLA Ops:
  14.5 10.4 %psum.7 = s32[]{:T(128)} all-reduce(s32[]{:T(128)} %reduce_sum.9), channel_id=1, replica_groups=mesh['rows'=16,'dict'=8] {'dict'}, use_global_device_ids=true, to_apply=%region_1.2 | all-reduce | flops 1 | bytes 8 | tf_op jit(solution)/shard_map/psum | solution.py:50
  26.6 7.4 %all-to-all-start.1 = ((s32[16,1,1]{2,1,0:T(1,128)}), s32[16,1,1]{2,1,0:T(1,128)S(1)}, u32[]{:S(2)}, u32[]{:S(2)}) async-start(s32[16,1,1]{2,1,0:T(1,128)} %broadcast_in_dim.291), calls=%async_computation.1 | async-start | bytes 16384 | tf_op jit(solution)/shard_map/all_to_all | solution.py:9
  68.7 5.8 %collective-permute-start.4 = (s32[16]{0:T(128)S(1)}, s32[16]{0:T(128)S(1)}, u32[]{:S(2)}, u32[]{:S(2)}) collective-permute-start(s32[16]{0:T(128)S(1)} %slice.274), channel_id=1, source_target_pairs={{1,0},{2,1},{3,2},{4,3},{5,4},{6,5},{7,6},{8,7},{9,8},{10,9},{11,1... | collective-permute-start | bytes 200 | tf_op jit(solution)/shard_map/ppermute | solution.py:37
  75.9 5.8 %collective-permute-start.5 = (s32[32]{0:T(128)S(1)}, s32[32]{0:T(128)S(1)}, u32[]{:S(2)}, u32[]{:S(2)}) collective-permute-start(s32[32]{0:T(128)S(1)} %slice.276), channel_id=1, source_target_pairs={{1,0},{2,1},{3,2},{4,3},{5,4},{6,5},{7,6},{8,7},{9,8},{10,9},{11,1... | collective-permute-start | bytes 392 | tf_op jit(solution)/shard_map/ppermute | solution.py:37
  88.9 7.7 %all-gather.2.cloned.1.call-done = bf16[65536,128]{1,0:T(8,128)(2,1)} async-done(((bf16[8192,128]{1,0:T(8,128)(2,1)}), bf16[65536,128]{1,0:T(8,128)(2,1)}) %all-gather.2.cloned.1.call-update) | async-done | bytes 16777232 | tf_op jit(solution)/shard_map/all_gather | solution.py:54
  96.5 19.0 %gather_fusion = bf16[4096,128]{1,0:T(8,128)(2,1)S(1)} fusion(bf16[65536,128]{1,0:T(8,128)(2,1)} %all-gather.2.cloned.1.call-done, s32[4096]{0:T(1024)S(1)} %fusion.21), kind=kCustom, calls=%fused_computation | custom fusion | bytes 2113536 | tf_op jit(solution)/shard_map/jit(_take)/gather | solution.py:55
  183.5 6.8 %broadcast_select_fusion.11 = (bf16[4096,128]{1,0:T(8,128)(2,1)S(1)}, bf16[4096,128]{1,0:T(8,128)(2,1)S(1)}) fusion(pred[4096]{0:T(1024)(128)(4,1)S(1)} %get-tuple-element.71, bf16[64,128]{1,0:T(8,128)(2,1)S(1)} %collective-permute-done.24, bf16[4032,128]{1,0:T(8,128)(2,1)S(1)} %slice.301, bf16[4096,128]{1,0:T(8,128)(2,1)S(1)} %get-tuple-element.44, ...), kind=kLoop, calls=%fused_computation.25 | loop fusion | flops 5767168 | bytes 5255168 | tf_op jit(solution)/shard_map/jit(_where)/select_n | solution.py:68
  207.6 8.0 %broadcast_select_fusion.9 = (bf16[4096,128]{1,0:T(8,128)(2,1)S(1)}, bf16[4096,128]{1,0:T(8,128)(2,1)S(1)}) fusion(pred[4096]{0:T(1024)(128)(4,1)S(1)} %get-tuple-element.73, bf16[256,128]{1,0:T(8,128)(2,1)S(1)} %collective-permute-done.26, bf16[3840,128]{1,0:T(8,128)(2,1)S(1)} %slice.305, bf16[4096,128]{1,0:T(8,128)(2,1)S(1)} %get-tuple-element.38, ...), kind=kLoop, calls=%fused_computation.23 | loop fusion | flops 5767168 | bytes 5255168 | tf_op jit(solution)/shard_map/jit(_where)/select_n | solution.py:68
  215.6 5.8 %collective-permute-start.27 = (bf16[512,128]{1,0:T(8,128)(2,1)S(1)}, bf16[512,128]{1,0:T(8,128)(2,1)S(1)}, u32[]{:S(2)}, u32[]{:S(2)}) collective-permute-start(bf16[512,128]{1,0:T(8,128)(2,1)S(1)} %slice.308), channel_id=1, source_target_pairs={{1,0},{2,1},{3,2},{4,3},{5,4},{6,5},{7,6},{8,7},{9,8},{10,9},{11,1... | collective-permute-start | bytes 393224 | tf_op jit(solution)/shard_map/ppermute | solution.py:37
  226.8 5.9 %collective-permute-start.28 = (bf16[1024,128]{1,0:T(8,128)(2,1)S(1)}, bf16[1024,128]{1,0:T(8,128)(2,1)S(1)}, u32[]{:S(2)}, u32[]{:S(2)}) collective-permute-start(bf16[1024,128]{1,0:T(8,128)(2,1)S(1)} %slice.310), channel_id=1, source_target_pairs={{1,0},{2,1},{3,2},{4,3},{5,4},{6,5},{7,6},{8,7},{9,8},{10,9},{11,1... | collective-permute-start | bytes 786440 | tf_op jit(solution)/shard_map/ppermute | solution.py:37
  236.8 10.4 %broadcast_select_fusion.7 = (bf16[4096,128]{1,0:T(8,128)(2,1)S(1)}, bf16[4096,128]{1,0:T(8,128)(2,1)S(1)}) fusion(pred[4096]{0:T(1024)(128)(4,1)S(1)} %get-tuple-element.75, bf16[1024,128]{1,0:T(8,128)(2,1)S(1)} %collective-permute-done.28, bf16[3072,128]{1,0:T(8,128)(2,1)S(1)} %slice.309, bf16[4096,128]{1,0:T(8,128)(2,1)S(1)} %get-tuple-element.32, ...), kind=kLoop, calls=%fused_computation.21 | loop fusion | flops 5767168 | bytes 5255168 | tf_op jit(solution)/shard_map/jit(_where)/select_n | solution.py:68
  247.2 5.9 %collective-permute-start.29 = (bf16[2048,128]{1,0:T(8,128)(2,1)S(1)}, bf16[2048,128]{1,0:T(8,128)(2,1)S(1)}, u32[]{:S(2)}, u32[]{:S(2)}) collective-permute-start(bf16[2048,128]{1,0:T(8,128)(2,1)S(1)} %get-tuple-element.60), channel_id=1, source_target_pairs={{1,0},{2,1},{3,2},{4,3},{5,4},{6,5},{7,6},{8,7},{9,8},{10,9},{11,1... | collective-permute-start | bytes 1572872 | tf_op jit(solution)/shard_map/ppermute | solution.py:37
  263.9 5.9 %collective-permute-start.30 = (bf16[4096,128]{1,0:T(8,128)(2,1)S(1)}, bf16[4096,128]{1,0:T(8,128)(2,1)S(1)}, u32[]{:S(2)}, u32[]{:S(2)}) collective-permute-start(bf16[4096,128]{1,0:T(8,128)(2,1)S(1)} %broadcast_select_fusion.6), channel_id=1, source_target_pairs={{1,0},{2,1},{3,2},{4,3},{5,4},{6,5},{7,6},{8,7},{9,8},{10,9},{11,1... | collective-permute-start | bytes 3145736 | tf_op jit(solution)/shard_map/ppermute | solution.py:37
  271.8 10.7 %collective-permute-done.13 = s32[4096]{0:T(1024)S(1)} collective-permute-done((s32[4096]{0:T(1024)S(1)}, s32[4096]{0:T(1024)S(1)}, u32[]{:S(2)}, u32[]{:S(2)}) %collective-permute-start.13) | collective-permute-done | bytes 16416 | tf_op jit(solution)/shard_map/ppermute | solution.py:37
  282.5 6.4 %broadcast_select_fusion.5 = (bf16[4096,128]{1,0:T(8,128)(2,1)S(1)}, bf16[4096,128]{1,0:T(8,128)(2,1)S(1)}) fusion(pred[4096]{0:T(1024)(128)(4,1)S(1)} %get-tuple-element.77, bf16[4096,128]{1,0:T(8,128)(2,1)S(1)} %collective-permute-done.30, bf16[4096,128]{1,0:T(8,128)(2,1)S(1)} %get-tuple-element.26, bf16[2048,128]{1,0:T(8,128)(2,1)S(1)} %collective-permute-done.29, ...), kind=kLoop, calls=%fused_computation.19 | loop fusion | flops 3670016 | bytes 5255168 | tf_op jit(solution)/shard_map/jit(_where)/select_n | solution.py:68
  288.9 6.5 %collective-permute-start.31 = (bf16[4096,128]{1,0:T(8,128)(2,1)S(1)}, bf16[4096,128]{1,0:T(8,128)(2,1)S(1)}, u32[]{:S(2)}, u32[]{:S(2)}) collective-permute-start(bf16[4096,128]{1,0:T(8,128)(2,1)S(1)} %get-tuple-element.19), channel_id=1, source_target_pairs={{2,0},{3,1},{4,2},{5,3},{6,4},{7,5},{8,6},{9,7},{10,8},{11,9},{12,... | collective-permute-start | bytes 3145736 | tf_op jit(solution)/shard_map/ppermute | solution.py:37
  297.4 20.8 %collective-permute-done.14 = s32[4096]{0:T(1024)S(1)} collective-permute-done((s32[4096]{0:T(1024)S(1)}, s32[4096]{0:T(1024)S(1)}, u32[]{:S(2)}, u32[]{:S(2)}) %collective-permute-start.14) | collective-permute-done | bytes 16416 | tf_op jit(solution)/shard_map/ppermute | solution.py:37
  319.7 6.8 %collective-permute-start.32 = (bf16[4096,128]{1,0:T(8,128)(2,1)S(1)}, bf16[4096,128]{1,0:T(8,128)(2,1)S(1)}, u32[]{:S(2)}, u32[]{:S(2)}) collective-permute-start(bf16[4096,128]{1,0:T(8,128)(2,1)S(1)} %broadcast_select_fusion.4), channel_id=1, source_target_pairs={{4,0},{5,1},{6,2},{7,3},{8,4},{9,5},{10,6},{11,7},{12,8},{13,9},{1... | collective-permute-start | bytes 3145736 | tf_op jit(solution)/shard_map/ppermute | solution.py:37
  328.8 21.0 %collective-permute-done.15 = s32[4096]{0:T(1024)S(1)} collective-permute-done((s32[4096]{0:T(1024)S(1)}, s32[4096]{0:T(1024)S(1)}, u32[]{:S(2)}, u32[]{:S(2)}) %collective-permute-start.15) | collective-permute-done | bytes 16416 | tf_op jit(solution)/shard_map/ppermute | solution.py:37
  357.6 39.3 %collective-permute-done.16 = s32[4096]{0:T(1024)S(1)} collective-permute-done((s32[4096]{0:T(1024)S(1)}, s32[4096]{0:T(1024)S(1)}, u32[]{:S(2)}, u32[]{:S(2)}) %collective-permute-start.16) | collective-permute-done | bytes 16416 | tf_op jit(solution)/shard_map/ppermute | solution.py:37
  396.9 11.5 %collective-permute-done.33 = bf16[4096,128]{1,0:T(8,128)(2,1)S(1)} collective-permute-done((bf16[4096,128]{1,0:T(8,128)(2,1)S(1)}, bf16[4096,128]{1,0:T(8,128)(2,1)S(1)}, u32[]{:S(2)}, u32[]{:S(2)}) %collective-permute-start.33) | collective-permute-done | bytes 1048608 | tf_op jit(solution)/shard_map/ppermute | solution.py:37
  413.0 20.3 %collective-permute-done.17 = s32[4096]{0:T(1024)S(1)} collective-permute-done((s32[4096]{0:T(1024)S(1)}, s32[4096]{0:T(1024)S(1)}, u32[]{:S(2)}, u32[]{:S(2)}) %collective-permute-start.17) | collective-permute-done | bytes 16416 | tf_op jit(solution)/shard_map/ppermute | solution.py:37
  438.1 25.7 %collective-permute-done.35 = bf16[4096,128]{1,0:T(8,128)(2,1)S(1)} collective-permute-done((bf16[4096,128]{1,0:T(8,128)(2,1)S(1)}, bf16[4096,128]{1,0:T(8,128)(2,1)S(1)}, u32[]{:S(2)}, u32[]{:S(2)}) %collective-permute-start.35) | collective-permute-done | bytes 1048608 | tf_op jit(solution)/shard_map/ppermute | solution.py:37
  466.4 26.3 %collective-permute-done.36 = bf16[4096,128]{1,0:T(8,128)(2,1)S(1)} collective-permute-done((bf16[4096,128]{1,0:T(8,128)(2,1)S(1)}, bf16[4096,128]{1,0:T(8,128)(2,1)S(1)}, u32[]{:S(2)}, u32[]{:S(2)}) %collective-permute-start.36) | collective-permute-done | bytes 1048608 | tf_op jit(solution)/shard_map/ppermute | solution.py:37
  (196 shorter events, 184.9 us)
Async XLA Ops:
  6.5 90.0 %all-gather.2.cloned.1.call-start = ((), (), s32[]{:S(2)}) async-start(), calls=%async_computation.2 | async-start | bytes 18874368 | tf_op jit(solution)/shard_map/all_gather | solution.py:54
  9.2 16.2 %all-to-all-start = ((s32[8,1,1]{2,1,0:T(1,128)}), s32[8,1,1]{2,1,0:T(1,128)S(1)}, u32[]{:S(2)}, u32[]{:S(2)}) async-start(s32[8,1,1]{2,1,0:T(1,128)} %broadcast_in_dim.289), calls=%async_computation | async-start | bytes 8192 | tf_op jit(solution)/shard_map/all_to_all | solution.py:9
  26.6 12.7 %all-to-all-start.1 = ((s32[16,1,1]{2,1,0:T(1,128)}), s32[16,1,1]{2,1,0:T(1,128)S(1)}, u32[]{:S(2)}, u32[]{:S(2)}) async-start(s32[16,1,1]{2,1,0:T(1,128)} %broadcast_in_dim.291), calls=%async_computation.1 | async-start | bytes 16384 | tf_op jit(solution)/shard_map/all_to_all | solution.py:9
  83.1 38.7 %collective-permute-start.6 = (s32[64]{0:T(128)S(1)}, s32[64]{0:T(128)S(1)}, u32[]{:S(2)}, u32[]{:S(2)}) collective-permute-start(s32[64]{0:T(128)S(1)} %slice.278), channel_id=1, source_target_pairs={{1,0},{2,1},{3,2},{4,3},{5,4},{6,5},{7,6},{8,7},{9,8},{10,9},{11,1... | collective-permute-start | bytes 776 | tf_op jit(solution)/shard_map/ppermute | solution.py:37
  127.3 8.0 %collective-permute-start.19 = (bf16[2,128]{1,0:T(2,128)(2,1)S(1)}, bf16[2,128]{1,0:T(2,128)(2,1)S(1)}, u32[]{:S(2)}, u32[]{:S(2)}) collective-permute-start(bf16[2,128]{1,0:T(2,128)(2,1)S(1)} %slice.292), channel_id=1, source_target_pairs={{1,0},{2,1},{3,2},{4,3},{5,4},{6,5},{7,6},{8,7},{9,8},{10,9},{11,1... | collective-permute-start | bytes 1544 | tf_op jit(solution)/shard_map/ppermute | solution.py:37
  133.0 8.4 %collective-permute-start.7 = (s32[128]{0:T(128)S(1)}, s32[128]{0:T(128)S(1)}, u32[]{:S(2)}, u32[]{:S(2)}) collective-permute-start(s32[128]{0:T(128)S(1)} %slice.280), channel_id=1, source_target_pairs={{1,0},{2,1},{3,2},{4,3},{5,4},{6,5},{7,6},{8,7},{9,8},{10,9},{11,1... | collective-permute-start | bytes 1544 | tf_op jit(solution)/shard_map/ppermute | solution.py:37
  152.5 8.4 %collective-permute-start.8 = (s32[256]{0:T(256)S(1)}, s32[256]{0:T(256)S(1)}, u32[]{:S(2)}, u32[]{:S(2)}) collective-permute-start(s32[256]{0:T(256)S(1)} %slice.282), channel_id=1, source_target_pairs={{1,0},{2,1},{3,2},{4,3},{5,4},{6,5},{7,6},{8,7},{9,8},{10,9},{11,1... | collective-permute-start | bytes 3080 | tf_op jit(solution)/shard_map/ppermute | solution.py:37
  172.9 9.2 %collective-permute-start.9 = (s32[512]{0:T(512)S(1)}, s32[512]{0:T(512)S(1)}, u32[]{:S(2)}, u32[]{:S(2)}) collective-permute-start(s32[512]{0:T(512)S(1)} %slice.284), channel_id=1, source_target_pairs={{1,0},{2,1},{3,2},{4,3},{5,4},{6,5},{7,6},{8,7},{9,8},{10,9},{11,1... | collective-permute-start | bytes 6152 | tf_op jit(solution)/shard_map/ppermute | solution.py:37
  196.1 9.6 %collective-permute-start.10 = (s32[1024]{0:T(1024)S(1)}, s32[1024]{0:T(1024)S(1)}, u32[]{:S(2)}, u32[]{:S(2)}) collective-permute-start(s32[1024]{0:T(1024)S(1)} %slice.286), channel_id=1, source_target_pairs={{1,0},{2,1},{3,2},{4,3},{5,4},{6,5},{7,6},{8,7},{9,8},{10,9},{11,1... | collective-permute-start | bytes 12296 | tf_op jit(solution)/shard_map/ppermute | solution.py:37
  215.6 8.3 %collective-permute-start.27 = (bf16[512,128]{1,0:T(8,128)(2,1)S(1)}, bf16[512,128]{1,0:T(8,128)(2,1)S(1)}, u32[]{:S(2)}, u32[]{:S(2)}) collective-permute-start(bf16[512,128]{1,0:T(8,128)(2,1)S(1)} %slice.308), channel_id=1, source_target_pairs={{1,0},{2,1},{3,2},{4,3},{5,4},{6,5},{7,6},{8,7},{9,8},{10,9},{11,1... | collective-permute-start | bytes 393224 | tf_op jit(solution)/shard_map/ppermute | solution.py:37
  226.8 9.9 %collective-permute-start.28 = (bf16[1024,128]{1,0:T(8,128)(2,1)S(1)}, bf16[1024,128]{1,0:T(8,128)(2,1)S(1)}, u32[]{:S(2)}, u32[]{:S(2)}) collective-permute-start(bf16[1024,128]{1,0:T(8,128)(2,1)S(1)} %slice.310), channel_id=1, source_target_pairs={{1,0},{2,1},{3,2},{4,3},{5,4},{6,5},{7,6},{8,7},{9,8},{10,9},{11,1... | collective-permute-start | bytes 786440 | tf_op jit(solution)/shard_map/ppermute | solution.py:37
  247.2 12.8 %collective-permute-start.29 = (bf16[2048,128]{1,0:T(8,128)(2,1)S(1)}, bf16[2048,128]{1,0:T(8,128)(2,1)S(1)}, u32[]{:S(2)}, u32[]{:S(2)}) collective-permute-start(bf16[2048,128]{1,0:T(8,128)(2,1)S(1)} %get-tuple-element.60), channel_id=1, source_target_pairs={{1,0},{2,1},{3,2},{4,3},{5,4},{6,5},{7,6},{8,7},{9,8},{10,9},{11,1... | collective-permute-start | bytes 1572872 | tf_op jit(solution)/shard_map/ppermute | solution.py:37
  263.9 18.6 %collective-permute-start.30 = (bf16[4096,128]{1,0:T(8,128)(2,1)S(1)}, bf16[4096,128]{1,0:T(8,128)(2,1)S(1)}, u32[]{:S(2)}, u32[]{:S(2)}) collective-permute-start(bf16[4096,128]{1,0:T(8,128)(2,1)S(1)} %broadcast_select_fusion.6), channel_id=1, source_target_pairs={{1,0},{2,1},{3,2},{4,3},{5,4},{6,5},{7,6},{8,7},{9,8},{10,9},{11,1... | collective-permute-start | bytes 3145736 | tf_op jit(solution)/shard_map/ppermute | solution.py:37
  269.8 12.6 %collective-permute-start.13 = (s32[4096]{0:T(1024)S(1)}, s32[4096]{0:T(1024)S(1)}, u32[]{:S(2)}, u32[]{:S(2)}) collective-permute-start(s32[4096]{0:T(1024)S(1)} %broadcast_select_fusion.30), channel_id=1, source_target_pairs={{2,0},{3,1},{4,2},{5,3},{6,4},{7,5},{8,6},{9,7},{10,8},{11,9},{12,... | collective-permute-start | bytes 49160 | tf_op jit(solution)/shard_map/ppermute | solution.py:37
  288.9 29.3 %collective-permute-start.31 = (bf16[4096,128]{1,0:T(8,128)(2,1)S(1)}, bf16[4096,128]{1,0:T(8,128)(2,1)S(1)}, u32[]{:S(2)}, u32[]{:S(2)}) collective-permute-start(bf16[4096,128]{1,0:T(8,128)(2,1)S(1)} %get-tuple-element.19), channel_id=1, source_target_pairs={{2,0},{3,1},{4,2},{5,3},{6,4},{7,5},{8,6},{9,7},{10,8},{11,9},{12,... | collective-permute-start | bytes 3145736 | tf_op jit(solution)/shard_map/ppermute | solution.py:37
  295.5 22.8 %collective-permute-start.14 = (s32[4096]{0:T(1024)S(1)}, s32[4096]{0:T(1024)S(1)}, u32[]{:S(2)}, u32[]{:S(2)}) collective-permute-start(s32[4096]{0:T(1024)S(1)} %broadcast_select_fusion.29), channel_id=1, source_target_pairs={{4,0},{5,1},{6,2},{7,3},{8,4},{9,5},{10,6},{11,7},{12,8},{13,9},{1... | collective-permute-start | bytes 49160 | tf_op jit(solution)/shard_map/ppermute | solution.py:37
  319.7 30.1 %collective-permute-start.32 = (bf16[4096,128]{1,0:T(8,128)(2,1)S(1)}, bf16[4096,128]{1,0:T(8,128)(2,1)S(1)}, u32[]{:S(2)}, u32[]{:S(2)}) collective-permute-start(bf16[4096,128]{1,0:T(8,128)(2,1)S(1)} %broadcast_select_fusion.4), channel_id=1, source_target_pairs={{4,0},{5,1},{6,2},{7,3},{8,4},{9,5},{10,6},{11,7},{12,8},{13,9},{1... | collective-permute-start | bytes 3145736 | tf_op jit(solution)/shard_map/ppermute | solution.py:37
  326.5 23.3 %collective-permute-start.15 = (s32[4096]{0:T(1024)S(1)}, s32[4096]{0:T(1024)S(1)}, u32[]{:S(2)}, u32[]{:S(2)}) collective-permute-start(s32[4096]{0:T(1024)S(1)} %broadcast_select_fusion.28), channel_id=1, source_target_pairs={{8,0},{9,1},{10,2},{11,3},{12,4},{13,5},{14,6},{15,7},{16,8},{17,9... | collective-permute-start | bytes 49160 | tf_op jit(solution)/shard_map/ppermute | solution.py:37
  353.2 55.2 %collective-permute-start.33 = (bf16[4096,128]{1,0:T(8,128)(2,1)S(1)}, bf16[4096,128]{1,0:T(8,128)(2,1)S(1)}, u32[]{:S(2)}, u32[]{:S(2)}) collective-permute-start(bf16[4096,128]{1,0:T(8,128)(2,1)S(1)} %get-tuple-element.13), channel_id=1, source_target_pairs={{8,0},{9,1},{10,2},{11,3},{12,4},{13,5},{14,6},{15,7},{16,8},{17,9... | collective-permute-start | bytes 3145736 | tf_op jit(solution)/shard_map/ppermute | solution.py:37
  355.6 41.2 %collective-permute-start.16 = (s32[4096]{0:T(1024)S(1)}, s32[4096]{0:T(1024)S(1)}, u32[]{:S(2)}, u32[]{:S(2)}) collective-permute-start(s32[4096]{0:T(1024)S(1)} %broadcast_select_fusion.27), channel_id=1, source_target_pairs={{16,0},{17,1},{18,2},{19,3},{20,4},{21,5},{22,6},{23,7},{24,8},{25... | collective-permute-start | bytes 49160 | tf_op jit(solution)/shard_map/ppermute | solution.py:37
  409.8 23.6 %collective-permute-start.34 = (bf16[4096,128]{1,0:T(8,128)(2,1)S(1)}, bf16[4096,128]{1,0:T(8,128)(2,1)S(1)}, u32[]{:S(2)}, u32[]{:S(2)}) collective-permute-start(bf16[4096,128]{1,0:T(8,128)(2,1)S(1)} %broadcast_select_fusion.2), channel_id=1, source_target_pairs={{16,0},{17,1},{18,2},{19,3},{20,4},{21,5},{22,6},{23,7},{24,8},{25... | collective-permute-start | bytes 3145736 | tf_op jit(solution)/shard_map/ppermute | solution.py:37
  411.7 21.6 %collective-permute-start.17 = (s32[4096]{0:T(1024)S(1)}, s32[4096]{0:T(1024)S(1)}, u32[]{:S(2)}, u32[]{:S(2)}) collective-permute-start(s32[4096]{0:T(1024)S(1)} %broadcast_select_fusion.26), channel_id=1, source_target_pairs={{32,0},{33,1},{34,2},{35,3},{36,4},{37,5},{38,6},{39,7},{40,8},{41... | collective-permute-start | bytes 49160 | tf_op jit(solution)/shard_map/ppermute | solution.py:37
  436.8 27.0 %collective-permute-start.35 = (bf16[4096,128]{1,0:T(8,128)(2,1)S(1)}, bf16[4096,128]{1,0:T(8,128)(2,1)S(1)}, u32[]{:S(2)}, u32[]{:S(2)}) collective-permute-start(bf16[4096,128]{1,0:T(8,128)(2,1)S(1)} %get-tuple-element.7), channel_id=1, source_target_pairs={{32,0},{33,1},{34,2},{35,3},{36,4},{37,5},{38,6},{39,7},{40,8},{41... | collective-permute-start | bytes 3145736 | tf_op jit(solution)/shard_map/ppermute | solution.py:37
  465.1 27.6 %collective-permute-start.36 = (bf16[4096,128]{1,0:T(8,128)(2,1)S(1)}, bf16[4096,128]{1,0:T(8,128)(2,1)S(1)}, u32[]{:S(2)}, u32[]{:S(2)}) collective-permute-start(bf16[4096,128]{1,0:T(8,128)(2,1)S(1)} %broadcast_select_fusion), channel_id=1, source_target_pairs={{64,0},{65,1},{66,2},{67,3},{68,4},{69,5},{70,6},{71,7},{72,8},{73... | collective-permute-start | bytes 3145736 | tf_op jit(solution)/shard_map/ppermute | solution.py:37
  (18 other events, 122.3 us)
Sparse Core Ops, SparseCore 0:
  9.0 87.4 all-gather.1
where the time goes:
time: 503 us; the launch traced here: 502 us
  waiting for transfers between devices  210 us (42%)
  starting transfers between devices  160 us (32%)
  other arithmetic  78.8 us (16%)
  local copies, waits for them, and re-layouts  26.3 us (5%)
  between operations  17 us (3%)
  blocking collectives  10.4 us (2%)
    ppermute x37, waiting for transfers between devices, from_behind(): return lax.ppermute(shard, axis, pairs)  199 us
    ppermute x37, starting transfers between devices, from_behind(): return lax.ppermute(shard, axis, pairs)  147 us
    select_n x19, other arithmetic, on_device(): send_values = jnp.where(moving[:, None], values, jnp.zeros_like(values))  72.9 us
    gather x1, local copies, waits for them, and re-layouts, on_device(): picked = jnp.take(whole, lookup_keys_per_record, axis=0)  19 us
    all_to_all x2, starting transfers between devices, sent_to_all(): lax.all_to_all(jnp.broadcast_to(shard[None], (size, *shard.shape)), axis,...  12.8 us
    psum x1, blocking collectives, on_device(): group_sum = lax.psum(kept_tally, 'dict')  10.4 us
  transfers between devices with their start and end apart: 40, of which 24 were waited for; matrix products, arithmetic and copies ran while one was open for 8% of the time, Pallas kernels for 0%

commit v1 on v0

v1 whole, which is shorter than its diff:
```python
import functools

import jax
import jax.numpy as jnp
from jax import lax
from jax.experimental import pallas as pl
from jax.experimental.pallas import tpu as pltpu
from jax.sharding import PartitionSpec as P

ALL = ("rows", "dict")
LANES = 128
PRESENT = 1 << 30
DEVICES = 128
BLOCKS = 32


def iota(shape, dim):
    return lax.broadcasted_iota(jnp.int32, shape, dim)


def exact_dot(a, b):
    return jnp.dot(a.astype(jnp.bfloat16), b.astype(jnp.bfloat16), preferred_element_type=jnp.float32)


def local_compaction(keys_ref, flags_ref, out_ref):
    flags = flags_ref[...]
    rows = flags.shape[0]
    upper = jnp.where(iota((LANES, LANES), 0) <= iota((LANES, LANES), 1), 1.0, 0.0)
    below = jnp.where(iota((rows, rows), 1) < iota((rows, rows), 0), 1.0, 0.0)
    kept = flags.astype(jnp.float32)
    inclusive = exact_dot(kept, upper)
    row_sums = exact_dot(kept, jnp.ones((LANES, LANES), jnp.float32))
    position = (inclusive + exact_dot(below, row_sums)).astype(jnp.int32) - 1
    count = jnp.sum(row_sums, axis=0, keepdims=True).astype(jnp.int32)
    here = iota((rows, LANES), 0) * LANES + iota((rows, LANES), 1)
    lane = iota((rows, LANES), 1)
    item = jnp.where(flags > 0, PRESENT | ((here - position) << 16) | keys_ref[...], 0)
    for level in range((rows * LANES - 1).bit_length()):
        step = 1 << level
        moving = (item >> (16 + level)) & 1 == 1
        sent = jnp.where(moving, item, 0)
        if step < LANES:
            near = pltpu.roll(sent, LANES - step, 1)
            arrived = jnp.where(lane < LANES - step, near, pltpu.roll(near, rows - 1, 0))
        else:
            arrived = pltpu.roll(sent, rows - step // LANES, 0)
        item = jnp.where(moving, 0, item) | arrived
    codes = item & 0xFFFF
    counts = jnp.broadcast_to(count, (LANES - rows, LANES))
    out_ref[...] = jnp.concatenate([codes, counts], axis=0).T


def regroup(me_ref, counts_ref, got_ref, out_ref, low_ref, high_ref, rows_ref):
    me = me_ref[0]
    got = got_ref[...]
    shape = got.shape
    lane = iota(shape, 1)
    count = jnp.max(jnp.where(lane >= BLOCKS, got, 0), axis=1, keepdims=True)
    count = jnp.broadcast_to(count, shape)
    below = jnp.where(iota(shape, 1) < iota(shape, 0), 1.0, 0.0)
    offset = 64 * exact_dot(below, (count >> 6).astype(jnp.float32)) + exact_dot(below, (count & 63).astype(jnp.float32))
    start = offset.astype(jnp.int32) + me
    valid = (lane < BLOCKS) & (lane * LANES + me < count)
    item = jnp.where(valid, PRESENT | ((start & 127) << 16) | got, 0)
    turn = (start >> 7) & (BLOCKS - 1)
    for level in range(5):
        item = jnp.where((turn >> level) & 1 == 1, pltpu.roll(item, 1 << level, 1), item)
    odd = iota(shape, 0) & 1 == 1
    low = jnp.where(lane < BLOCKS, item, 0)
    high = jnp.where(lane < BLOCKS, pltpu.roll(item, LANES - BLOCKS, 1), 0)
    low_ref[...] = jnp.where(odd, pltpu.roll(low, BLOCKS, 1), low)
    high_ref[...] = jnp.where(odd, pltpu.roll(high, BLOCKS, 1), high)
    rows_ref[...] = jnp.zeros_like(rows_ref)

    def place(s, before):
        d = (before + me) >> 12
        rows_ref[pl.ds(d, 1), :] = rows_ref[pl.ds(d, 1), :] | low_ref[pl.ds(s, 1), :]
        rows_ref[pl.ds(d + 1, 1), :] = rows_ref[pl.ds(d + 1, 1), :] | high_ref[pl.ds(s, 1), :]
        return before + counts_ref[s]

    lax.fori_loop(0, DEVICES, place, jnp.int32(0), unroll=8)
    out_ref[...] = rows_ref[:DEVICES, :]


def placement(got_ref, out_ref, *, absent):
    item = got_ref[...].T[: 2 * BLOCKS]
    lane = iota(item.shape, 1)
    turn = (((item >> 16) & 127) - lane) & 127
    item = jnp.where(item > 0, (item & (PRESENT | 0xFFFF)) | (turn << 16), 0)
    for level in range(7):
        moving = (item >> (16 + level)) & 1 == 1
        item = jnp.where(moving, 0, item) | pltpu.roll(jnp.where(moving, item, 0), 1 << level, 1)
    item = item[:BLOCKS] | item[BLOCKS:]
    out_ref[...] = jnp.where(item > 0, item & 0xFFFF, absent)


def decode(codes_ref, table_ref, out_ref, wide_ref, part_ref, staged_ref, sems):
    entries = table_ref.shape[0]
    slots, chunk = part_ref.shape[:2]
    chunks = entries // chunk

    def fetch(c):
        return pltpu.make_async_copy(
            table_ref.at[pl.ds(c * chunk, chunk)], part_ref.at[c % slots], sems.at[c % slots]
        )

    for c in range(slots):
        fetch(c).start()
    wide_ref[pl.ds(entries, 8), :] = jnp.zeros((8, LANES), jnp.float32)
    for c in range(chunks):
        fetch(c).wait()

        def widen(i, _, c=c):
            at = pl.multiple_of(i * 128, 128)
            to = pl.multiple_of(c * chunk + i * 128, 128)
            wide_ref[pl.ds(to, 128), :] = part_ref[c % slots, pl.ds(at, 128), :].astype(jnp.float32)
            return 0

        lax.fori_loop(0, chunk // 128, widen, 0)
        if c + slots < chunks:
            fetch(c + slots).start()

    def block(b, _):
        base = pl.multiple_of(b * LANES, LANES)
        for j in range(LANES):
            staged_ref[pl.ds(j, 1), :] = wide_ref[pl.ds(codes_ref[b, j], 1), :]
        out_ref[pl.ds(base, LANES), :] = staged_ref[...].astype(out_ref.dtype)
        return 0

    lax.fori_loop(0, BLOCKS, block, 0)


def vmem():
    return pl.BlockSpec(memory_space=pltpu.VMEM)


def smem():
    return pl.BlockSpec(memory_space=pltpu.SMEM)


def exchange(x):
    return lax.all_to_all(x, ALL, 0, 0, tiled=True)


def on_device(lookup_keys_per_record, filter_passed_flags, decoding_table):
    me = lax.axis_index(ALL).astype(jnp.int32).reshape(1)
    square = jax.ShapeDtypeStruct((DEVICES, LANES), jnp.int32)
    whole = lax.all_gather(decoding_table, "dict", axis=0, tiled=True)
    sent = pl.pallas_call(local_compaction, out_shape=square, in_specs=[vmem(), vmem()], out_specs=vmem(), name="local_compaction")(
        lookup_keys_per_record.reshape(BLOCKS, LANES), filter_passed_flags.reshape(BLOCKS, LANES)
    )
    got = exchange(sent)
    sent = pl.pallas_call(
        regroup,
        out_shape=square,
        in_specs=[smem(), smem(), vmem()],
        out_specs=vmem(),
        scratch_shapes=[pltpu.VMEM((DEVICES, LANES), jnp.int32)] * 2 + [pltpu.VMEM((DEVICES + 8, LANES), jnp.int32)],
        name="regroup",
    )(me, got[:, BLOCKS], got)
    got = exchange(sent)
    entries = whole.shape[0]
    codes = pl.pallas_call(
        functools.partial(placement, absent=entries),
        out_shape=jax.ShapeDtypeStruct((BLOCKS, LANES), jnp.int32),
        in_specs=[vmem()],
        out_specs=vmem(),
        name="placement",
    )(got)
    return pl.pallas_call(
        decode,
        out_shape=jax.ShapeDtypeStruct((BLOCKS * LANES, LANES), jnp.bfloat16),
        in_specs=[smem(), pl.BlockSpec(memory_space=pl.ANY)],
        out_specs=vmem(),
        scratch_shapes=[
            pltpu.VMEM((entries + 8, LANES), jnp.float32),
            pltpu.VMEM((4, 4096, LANES), jnp.bfloat16),
            pltpu.VMEM((LANES, LANES), jnp.float32),
            pltpu.SemaphoreType.DMA((4,)),
        ],
        compiler_params=pltpu.CompilerParams(vmem_limit_bytes=48 << 20),
        name="decode",
    )(codes, whole)


def solution(mesh):
    placed = (P(ALL), P(ALL), P("dict", None))
    return jax.shard_map(
        on_device, mesh=mesh, in_specs=placed, out_specs=P(ALL, None), check_vma=False
    )
```

time: 503 us -> 120 us (0.24)
  waiting for transfers between devices: 210 us -> 56.8 us
  starting transfers between devices: 160 us -> 10.5 us
  other arithmetic: 78.8 us -> 0 us
  local copies, waits for them, and re-layouts: 26.3 us -> 1.42 us
  Pallas kernels: 0 us -> 20.7 us
    ppermute x37 -> x0, waiting for transfers between devices: 199 us -> none  [from_behind(): return lax.ppermute(shard, axis, pairs)]
    ppermute x37 -> x0, starting transfers between devices: 147 us -> none  [from_behind(): return lax.ppermute(shard, axis, pairs)]
    select_n x40 -> x0, other arithmetic: 75.6 us -> none  [the longest x19 72.9 us: on_device(): send_values = jnp.where(moving[:, None], values, jnp.zeros_like(values))]
    all_gather x1, waiting for transfers between devices: 7.66 us -> 48.1 us  [on_device(): whole = lax.all_gather(decoding_table, 'dict', axis=0, tiled=True)]
    pallas_call x0 -> x4, Pallas kernels: none -> 20.7 us  [the longest x1 13.1 us: on_device(): pl.pallas_call(decode, out_shape=jax.ShapeDtypeStruct((BLOCKS * LANES, LA...]
    gather x1 -> x0, local copies, waits for them, and re-layouts: 19 us -> none  [on_device(): picked = jnp.take(whole, lookup_keys_per_record, axis=0)]
    all_to_all x0 -> x1, blocking collectives: none -> 15.3 us  [exchange(): return lax.all_to_all(x, ALL, 0, 0, tiled=True)]
    psum x1 -> x0, blocking collectives: 10.4 us -> none  [on_device(): group_sum = lax.psum(kept_tally, 'dict')]
  transfers between devices with their start and end apart: 40 -> 2, of which waited for: 24 -> 2; matrix products, arithmetic and copies ran while one was open for 8% -> 1% of each run, Pallas kernels for 0% -> 6%
where the time goes in v1:
time: 120 us; the launch traced here: 118 us
  waiting for transfers between devices  56.8 us (47%)
  Pallas kernels  20.7 us (17%)
  blocking collectives  15.3 us (13%)
  between operations  13.4 us (11%)
  starting transfers between devices  10.5 us (9%)
  local copies, waits for them, and re-layouts  1.42 us (1%)
    all_gather x1, waiting for transfers between devices, on_device(): whole = lax.all_gather(decoding_table, 'dict', axis=0, tiled=True)  48.1 us
    all_to_all x1, blocking collectives, exchange(): return lax.all_to_all(x, ALL, 0, 0, tiled=True)  15.3 us
    pallas_call x1, Pallas kernels, on_device(): pl.pallas_call(decode, out_shape=jax.ShapeDtypeStruct((BLOCKS * LANES, LA...  13.1 us
    all_to_all x1, starting transfers between devices, exchange(): return lax.all_to_all(x, ALL, 0, 0, tiled=True)  10.5 us
    all_to_all x1, waiting for transfers between devices, exchange(): return lax.all_to_all(x, ALL, 0, 0, tiled=True)  8 us
    pallas_call x1, Pallas kernels, on_device(): pl.pallas_call(regroup, out_shape=square, in_specs=[smem(), smem(), vmem(...  3.19 us
  transfers between devices with their start and end apart: 2, of which 2 were waited for; matrix products, arithmetic and copies ran while one was open for 1% of the time, Pallas kernels for 6%

profile of v1, /device:TPU:4, one launch (start us, length us, event | category | flops | bytes accessed | tf_op | source)
XLA Modules:
  0.0 118.1 jit_solution(13114816513785383563)
XLA Ops:
  6.5 0.0 all-gather.2.cloned.1.call-start
  6.5 0.7 all-gather.2.cloned.1.call-update
  7.3 2.3 %local_compaction.1 = s32[128,128]{1,0:T(8,128)} custom-call(s32[32,128]{1,0:T(8,128)} %bitcast.16, s32[32,128]{1,0:T(8,128)} %bitcast.17), custom_call_target="tpu_custom_call" | custom-call | tf_op jit(solution)/shard_map/local_compaction/pallas_call | solution.py:149
  9.6 10.5 %all-to-all-start = ((s32[128,1,128]{2,1,0:T(1,128)}), s32[128,1,128]{2,1,0:T(1,128)S(1)}, u32[]{:S(2)}, u32[]{:S(2)}) async-start(s32[128,1,128]{2,1,0:T(1,128)} %bitcast.14), calls=%async_computation | async-start | bytes 131072 | tf_op jit(solution)/shard_map/all_to_all | solution.py:142
  20.1 8.0 %all-to-all-done = s32[128,1,128]{2,1,0:T(1,128)S(1)} async-done(((s32[128,1,128]{2,1,0:T(1,128)}), s32[128,1,128]{2,1,0:T(1,128)S(1)}, u32[]{:S(2)}, u32[]{:S(2)}) %all-to-all-start) | async-done | bytes 65568 | tf_op jit(solution)/shard_map/all_to_all | solution.py:142
  28.1 0.0 copy-start.1
  28.1 0.7 slice_reduce_fusion.counts_ref
  28.8 0.0 copy-done.1
  28.8 3.2 %regroup.1 = s32[128,128]{1,0:T(8,128)} custom-call(s32[1]{0:T(128)} %bitcast.me_ref, s32[128]{0:T(128)} %slice_reduce_fusion.counts_ref, s32[128,128]{1,0:T(8,128)} %bitcast.12), custom_call_target="tpu_custom_call" | custom-call | tf_op jit(solution)/shard_map/regroup/pallas_call | solution.py:153
  32.0 15.3 %all_to_all.22 = s32[128,1,128]{2,1,0:T(1,128)} all-to-all(s32[128,1,128]{2,1,0:T(1,128)} %bitcast.15), channel_id=1, replica_groups=mesh['rows'=16,'dict'=8] {'rows','dict'}, dimensions={0} | all-to-all | bytes 131072 | tf_op jit(solution)/shard_map/all_to_all | solution.py:142
  47.2 2.0 %placement.1.codes_ref = s32[32,128]{1,0:T(8,128)} custom-call(s32[128,128]{1,0:T(8,128)} %bitcast.13), custom_call_target="tpu_custom_call" | custom-call | tf_op jit(solution)/shard_map/placement/pallas_call | solution.py:163
  49.3 48.1 %all-gather.2.cloned.1.call-done.table_ref = bf16[65536,128]{1,0:T(8,128)(2,1)} async-done(((bf16[8192,128]{1,0:T(8,128)(2,1)}), bf16[65536,128]{1,0:T(8,128)(2,1)}) %all-gather.2.cloned.1.call-update) | async-done | bytes 16777232 | tf_op jit(solution)/shard_map/all_gather | solution.py:148
  97.4 0.0 copy-start
  97.4 0.7 copy-done
  98.1 13.1 %decode.1 = bf16[4096,128]{1,0:T(8,128)(2,1)} custom-call(s32[32,128]{1,0:T(8,128)S(1)} %copy-done, bf16[65536,128]{1,0:T(8,128)(2,1)} %all-gather.2.cloned.1.call-done.table_ref), custom_call_target="tpu_custom_call" | custom-call | tf_op jit(solution)/shard_map/decode/pallas_call | solution.py:170
Async XLA Ops:
  6.5 90.8 %all-gather.2.cloned.1.call-start = ((), (), s32[]{:S(2)}) async-start(), calls=%async_computation.2 | async-start | bytes 18874368 | tf_op jit(solution)/shard_map/all_gather | solution.py:148
  9.6 18.5 %all-to-all-start = ((s32[128,1,128]{2,1,0:T(1,128)}), s32[128,1,128]{2,1,0:T(1,128)S(1)}, u32[]{:S(2)}, u32[]{:S(2)}) async-start(s32[128,1,128]{2,1,0:T(1,128)} %bitcast.14), calls=%async_computation | async-start | bytes 131072 | tf_op jit(solution)/shard_map/all_to_all | solution.py:142
  28.1 0.7 copy-start.1
  97.4 0.7 copy-start
Sparse Core Ops, SparseCore 0:
  9.0 88.2 all-gather.1

commit v2 on v1

--- a/solution.py
+++ b/solution.py
@@ -1,5 +1,3 @@
-import functools
-
 import jax
 import jax.numpy as jnp
 from jax import lax
@@ -7,11 +5,18 @@
 from jax.experimental.pallas import tpu as pltpu
 from jax.sharding import PartitionSpec as P
 
+
 ALL = ("rows", "dict")
 LANES = 128
 PRESENT = 1 << 30
 DEVICES = 128
 BLOCKS = 32
+SHARD = 8192
+PART = 768
+HALF = PART // 2
+REST = SHARD - 8 * PART
+ENTRIES = 8 * SHARD
+RING = (2, -1, 1)
 
 
 def iota(shape, dim):
@@ -82,7 +87,44 @@
     out_ref[...] = rows_ref[:DEVICES, :]
 
 
-def placement(got_ref, out_ref, *, absent):
+def colours(x, y):
+    return (x + 2 * y) & 3, (2 * x + y) & 3
+
+
+def table_parts(me, half):
+    x, y, z, core = (me >> 3) & 3, me >> 5, (me >> 1) & 3, (me & 1) ^ half
+    a, b = colours(x, y)
+    bases = [(((z + step) & 3) * 2 + core) * SHARD for step in RING]
+
+    def first(colour, at=0):
+        return PART * (colour & 3) + at
+
+    def second(colour, at=0):
+        return PART * (4 + (colour & 3)) + at
+
+    def pieces(whole, part):
+        return [(PART, base + whole) for base in bases] + [(HALF, base + part) for base in bases]
+
+    parts = [[(SHARD, (z * 2 + core) * SHARD)]]
+    parts += [[(PART, base + at) for base in bases for at in (first(a), second(b))]]
+    parts += [[(REST, base + 8 * PART)] for base in bases]
+    parts += [pieces(first(a - 1), second(b + 2)), pieces(first(a + 1), second(b + 2, HALF))]
+    parts += [pieces(second(b - 1), first(a + 2)), pieces(second(b + 1), first(a + 2, HALF))]
+    return parts
+
+
+def decode(me_ref, got_ref, *refs):
+    pieces, (out_ref, table_ref, pairs_ref, wide_ref, place_ref, scalar_ref, sem, place_sem) = refs[:-8], refs[-8:]
+    me = me_ref[0]
+    for piece, places in zip(pieces, table_parts(me, 0) + table_parts(me, 1)):
+        at = 0
+        for rows, base in places:
+            pltpu.make_async_copy(
+                piece.at[pl.ds(at // 2, rows // 2)], table_ref.at[pl.ds(base >> 1, rows // 2)], sem
+            ).start()
+            at += rows
+    table_ref[pl.ds(ENTRIES // 2, 8)] = jnp.zeros((8, 2, LANES), table_ref.dtype)
+
     item = got_ref[...].T[: 2 * BLOCKS]
     lane = iota(item.shape, 1)
     turn = (((item >> 16) & 127) - lane) & 127
@@ -91,43 +133,103 @@
         moving = (item >> (16 + level)) & 1 == 1
         item = jnp.where(moving, 0, item) | pltpu.roll(jnp.where(moving, item, 0), 1 << level, 1)
     item = item[:BLOCKS] | item[BLOCKS:]
-    out_ref[...] = jnp.where(item > 0, item & 0xFFFF, absent)
-
-
-def decode(codes_ref, table_ref, out_ref, wide_ref, part_ref, staged_ref, sems):
-    entries = table_ref.shape[0]
-    slots, chunk = part_ref.shape[:2]
-    chunks = entries // chunk
-
-    def fetch(c):
-        return pltpu.make_async_copy(
-            table_ref.at[pl.ds(c * chunk, chunk)], part_ref.at[c % slots], sems.at[c % slots]
-        )
-
-    for c in range(slots):
-        fetch(c).start()
-    wide_ref[pl.ds(entries, 8), :] = jnp.zeros((8, LANES), jnp.float32)
-    for c in range(chunks):
-        fetch(c).wait()
-
-        def widen(i, _, c=c):
-            at = pl.multiple_of(i * 128, 128)
-            to = pl.multiple_of(c * chunk + i * 128, 128)
-            wide_ref[pl.ds(to, 128), :] = part_ref[c % slots, pl.ds(at, 128), :].astype(jnp.float32)
-            return 0
-
-        lax.fori_loop(0, chunk // 128, widen, 0)
-        if c + slots < chunks:
-            fetch(c + slots).start()
-
-    def block(b, _):
-        base = pl.multiple_of(b * LANES, LANES)
+    place_ref[...] = jnp.where(item > 0, (item & 0xFFFF) >> 1, ENTRIES // 2)
+    to_scalars = pltpu.make_async_copy(place_ref, scalar_ref, place_sem)
+    to_scalars.start()
+    odd = jnp.concatenate([item & 1, jnp.zeros((LANES - BLOCKS, LANES), jnp.int32)], axis=0).T
+    to_scalars.wait()
+    filled = table_ref.at[pl.ds(0, ENTRIES // 2)]
+    pltpu.make_async_copy(filled, filled, sem).wait()
+
+    def fetch(b, _):
         for j in range(LANES):
-            staged_ref[pl.ds(j, 1), :] = wide_ref[pl.ds(codes_ref[b, j], 1), :]
-        out_ref[pl.ds(base, LANES), :] = staged_ref[...].astype(out_ref.dtype)
+            pairs_ref[b, 2 * j : 2 * j + 2, :] = table_ref[scalar_ref[b, j]]
         return 0
 
-    lax.fori_loop(0, BLOCKS, block, 0)
+    lax.fori_loop(0, BLOCKS, fetch, 0)
+    for b in range(BLOCKS):
+        wide = wide_ref.at[b % 4]
+        wide[...] = pairs_ref[b].astype(jnp.float32)
+        second = jnp.broadcast_to(odd[:, b : b + 1], (LANES, LANES)) == 1
+        row = jnp.where(second, wide[pl.ds(1, LANES, stride=2), :], wide[pl.ds(0, LANES, stride=2), :])
+        out_ref[b * LANES : (b + 1) * LANES, :] = row.astype(out_ref.dtype)
+
+
+def moved(x, by):
+    pairs = []
+    for me in range(DEVICES):
+        place = ((me >> 3) & 3, me >> 5, (me >> 1) & 3, me & 1)
+        to_x, to_y, to_z, to_core = by(*place)
+        pairs.append((me, ((to_y & 3) * 4 + (to_x & 3)) * 8 + (to_z & 3) * 2 + to_core))
+    return lax.ppermute(x, ALL, pairs)
+
+
+def along_z(piece):
+    return [moved(piece, lambda x, y, z, core, step=step: (x, y, z - step, core)) for step in RING]
+
+
+def other_core(piece):
+    return moved(piece, lambda x, y, z, core: (x, y, z, 1 - core))
+
+
+def cut(me_ref, table_ref, parts_ref, rest_ref, sems):
+    a, b = colours((me_ref[0] >> 3) & 3, me_ref[0] >> 5)
+    copies = [
+        pltpu.make_async_copy(table_ref.at[pl.ds(PART * a, PART)], parts_ref.at[pl.ds(0, PART)], sems.at[0]),
+        pltpu.make_async_copy(table_ref.at[pl.ds(PART * (4 + b), PART)], parts_ref.at[pl.ds(PART, PART)], sems.at[1]),
+        pltpu.make_async_copy(table_ref.at[pl.ds(8 * PART, REST)], rest_ref, sems.at[2]),
+    ]
+    for copy in copies:
+        copy.start()
+    for copy in copies:
+        copy.wait()
+
+
+def join(*refs):
+    pieces, joined, all_ref = refs[: len(RING)], refs[len(RING) : -1], refs[-1]
+    for out, (whole, part) in zip(joined, ((0, PART), (0, PART + HALF), (PART, 0), (PART, HALF))):
+        for k, piece in enumerate(pieces):
+            out[PART * k : PART * (k + 1), :] = piece[whole : whole + PART, :]
+            to = PART * len(RING) + HALF * k
+            out[to : to + HALF, :] = piece[part : part + HALF, :]
+    for k, piece in enumerate(pieces):
+        all_ref[2 * PART * k : 2 * PART * (k + 1), :] = piece[...]
+
+
+def first_pieces(me, table):
+    parts, rest = pl.pallas_call(
+        cut,
+        out_shape=[pltpu.VMEM((rows, LANES), table.dtype) for rows in (2 * PART, REST)],
+        in_specs=[smem(), anywhere()],
+        out_specs=[vmem()] * 2,
+        scratch_shapes=[pltpu.SemaphoreType.DMA((3,))],
+        name="cut",
+    )(me, table)
+    first = along_z(parts)
+    rest = along_z(rest)
+    return first, rest
+
+
+def ring_pieces(first):
+    rows = len(RING) * (PART + HALF)
+    *sent, every = pl.pallas_call(
+        join,
+        out_shape=[pltpu.VMEM((rows, LANES), first[0].dtype)] * 4
+        + [jax.ShapeDtypeStruct((2 * PART * len(RING), LANES), first[0].dtype)],
+        in_specs=[vmem()] * len(first),
+        out_specs=[vmem()] * 5,
+        name="join",
+    )(*first)
+    return every, [
+        moved(sent[0], lambda x, y, z, core: (x + 1, y, z, core)),
+        moved(sent[1], lambda x, y, z, core: (x - 1, y, z, core)),
+        moved(sent[2], lambda x, y, z, core: (x, y + 1, z, core)),
+        moved(sent[3], lambda x, y, z, core: (x, y - 1, z, core)),
+    ]
+
+
+def anywhere():
+    return pl.BlockSpec(memory_space=pl.ANY)
 
 
 def vmem():
@@ -142,14 +244,17 @@
     return lax.all_to_all(x, ALL, 0, 0, tiled=True)
 
 
-def on_device(lookup_keys_per_record, filter_passed_flags, decoding_table):
+def steps(lookup_keys_per_record, filter_passed_flags, decoding_table):
     me = lax.axis_index(ALL).astype(jnp.int32).reshape(1)
     square = jax.ShapeDtypeStruct((DEVICES, LANES), jnp.int32)
-    whole = lax.all_gather(decoding_table, "dict", axis=0, tiled=True)
+    first, rest = first_pieces(me, decoding_table)
+    other_table = other_core(decoding_table)
     sent = pl.pallas_call(local_compaction, out_shape=square, in_specs=[vmem(), vmem()], out_specs=vmem(), name="local_compaction")(
         lookup_keys_per_record.reshape(BLOCKS, LANES), filter_passed_flags.reshape(BLOCKS, LANES)
     )
     got = exchange(sent)
+    every, ring = ring_pieces(first)
+    other_every = other_core(every)
     sent = pl.pallas_call(
         regroup,
         out_shape=square,
@@ -159,32 +264,29 @@
         name="regroup",
     )(me, got[:, BLOCKS], got)
     got = exchange(sent)
-    entries = whole.shape[0]
-    codes = pl.pallas_call(
-        functools.partial(placement, absent=entries),
-        out_shape=jax.ShapeDtypeStruct((BLOCKS, LANES), jnp.int32),
-        in_specs=[vmem()],
-        out_specs=vmem(),
-        name="placement",
-    )(got)
+    other_rest = [other_core(piece) for piece in rest]
+    other_ring = [other_core(piece) for piece in ring]
+    pieces = [decoding_table, every, *rest, *ring, other_table, other_every, *other_rest, *other_ring]
+    pieces = [pltpu.with_memory_space_constraint(piece.reshape(-1, 2, LANES), pltpu.HBM) for piece in pieces]
     return pl.pallas_call(
         decode,
         out_shape=jax.ShapeDtypeStruct((BLOCKS * LANES, LANES), jnp.bfloat16),
-        in_specs=[smem(), pl.BlockSpec(memory_space=pl.ANY)],
+        in_specs=[smem(), vmem()] + [anywhere()] * len(pieces),
         out_specs=vmem(),
         scratch_shapes=[
-            pltpu.VMEM((entries + 8, LANES), jnp.float32),
-            pltpu.VMEM((4, 4096, LANES), jnp.bfloat16),
-            pltpu.VMEM((LANES, LANES), jnp.float32),
-            pltpu.SemaphoreType.DMA((4,)),
+            pltpu.VMEM((ENTRIES // 2 + 8, 2, LANES), jnp.bfloat16),
+            pltpu.VMEM((BLOCKS, 2 * LANES, LANES), jnp.bfloat16),
+            pltpu.VMEM((4, 2 * LANES, LANES), jnp.float32),
+            pltpu.VMEM((BLOCKS, LANES), jnp.int32),
+            pltpu.SMEM((BLOCKS, LANES), jnp.int32),
+            pltpu.SemaphoreType.DMA(()),
+            pltpu.SemaphoreType.DMA(()),
         ],
-        compiler_params=pltpu.CompilerParams(vmem_limit_bytes=48 << 20),
+        compiler_params=pltpu.CompilerParams(vmem_limit_bytes=32 << 20),
         name="decode",
-    )(codes, whole)
+    )(me, got, *pieces)
 
 
 def solution(mesh):
     placed = (P(ALL), P(ALL), P("dict", None))
-    return jax.shard_map(
-        on_device, mesh=mesh, in_specs=placed, out_specs=P(ALL, None), check_vma=False
-    )
+    return jax.shard_map(steps, mesh=mesh, in_specs=placed, out_specs=P(ALL, None), check_vma=False)

time: 120 us -> 131 us (1.092)
  the two profiles are of different devices: /device:TPU:4 before, /device:TPU:1 now
where the time goes in v2:
time: 131 us
  waiting for transfers between devices  47.9 us (37%)
  blocking collectives  31.7 us (24%)
  starting transfers between devices  25.6 us (20%)
  Pallas kernels  22.1 us (17%)
  local copies, waits for them, and re-layouts  3.58 us (3%)
    ppermute x19, waiting for transfers between devices, moved(): return lax.ppermute(x, ALL, pairs)  47.9 us
    all_to_all x2, blocking collectives, exchange(): return lax.all_to_all(x, ALL, 0, 0, tiled=True)  31.7 us
    ppermute x19, starting transfers between devices, moved(): return lax.ppermute(x, ALL, pairs)  25.6 us
    pallas_call x1, Pallas kernels, steps(): pl.pallas_call(decode, out_shape=jax.ShapeDtypeStruct((BLOCKS * LANES, LA...  12.1 us
    pallas_call x1, Pallas kernels, steps(): pl.pallas_call(regroup, out_shape=square, in_specs=[smem(), smem(), vmem(...  3.2 us
    unnamed x20, local copies, waits for them, and re-layouts  2.84 us
  transfers between devices with their start and end apart: 19, of which 7 were waited for; matrix products, arithmetic and copies ran while one was open for 1% of the time, Pallas kernels for 6%

profile of v2, /device:TPU:1, one launch (start us, length us, event | category | flops | bytes accessed | tf_op | source)
XLA Modules:
  0.0 131.1 jit_solution(13606167772922172432)
XLA Ops:
  0.0 2.1 %cut.1 = (bf16[1536,128]{1,0:T(8,128)(2,1)S(1)}, bf16[2048,128]{1,0:T(8,128)(2,1)}) custom-call(s32[1]{0:T(128)} %bitcast.me_ref, bf16[8192,128]{1,0:T(8,128)(2,1)} %table_ref.1), custom_call_target="tpu_custom_call" | custom-call | tf_op jit(solution)/shard_map/cut/pallas_call | solution.py:200
  2.1 4.6 %collective-permute-start.2 = (bf16[1536,128]{1,0:T(8,128)(2,1)S(1)}, bf16[1536,128]{1,0:T(8,128)(2,1)S(1)}, u32[]{:S(2)}, u32[]{:S(2)}) collective-permute-start(bf16[1536,128]{1,0:T(8,128)(2,1)S(1)} %get-tuple-element.12), channel_id=1, source_target_pairs={{0,6},{1,7},{2,0},{3,1},{4,2},{5,3},{6,4},{7,5},{8,14},{9,15},{10,... | collective-permute-start | bytes 1179656 | tf_op jit(solution)/shard_map/ppermute | solution.py:164
  6.8 1.3 %collective-permute-start.1 = (bf16[1536,128]{1,0:T(8,128)(2,1)S(1)}, bf16[1536,128]{1,0:T(8,128)(2,1)S(1)}, u32[]{:S(2)}, u32[]{:S(2)}) collective-permute-start(bf16[1536,128]{1,0:T(8,128)(2,1)S(1)} %get-tuple-element.12), channel_id=1, source_target_pairs={{0,2},{1,3},{2,4},{3,5},{4,6},{5,7},{6,0},{7,1},{8,10},{9,11},{10,... | collective-permute-start | bytes 1179656 | tf_op jit(solution)/shard_map/ppermute | solution.py:164
  8.2 1.9 %collective-permute-start.4 = (bf16[2048,128]{1,0:T(8,128)(2,1)}, bf16[2048,128]{1,0:T(8,128)(2,1)}, u32[]{:S(2)}, u32[]{:S(2)}) collective-permute-start(bf16[2048,128]{1,0:T(8,128)(2,1)} %get-tuple-element.14), channel_id=1, source_target_pairs={{0,2},{1,3},{2,4},{3,5},{4,6},{5,7},{6,0},{7,1},{8,10},{9,11},{10,... | collective-permute-start | bytes 1572872 | tf_op jit(solution)/shard_map/ppermute | solution.py:164
  10.1 4.4 %collective-permute-done.2.refs_2_ = bf16[1536,128]{1,0:T(8,128)(2,1)S(1)} collective-permute-done((bf16[1536,128]{1,0:T(8,128)(2,1)S(1)}, bf16[1536,128]{1,0:T(8,128)(2,1)S(1)}, u32[]{:S(2)}, u32[]{:S(2)}) %collective-permute-start.2) | collective-permute-done | bytes 393248 | tf_op jit(solution)/shard_map/ppermute | solution.py:164
  14.5 2.0 %collective-permute-start.3 = (bf16[2048,128]{1,0:T(8,128)(2,1)}, bf16[2048,128]{1,0:T(8,128)(2,1)}, u32[]{:S(2)}, u32[]{:S(2)}) collective-permute-start(bf16[2048,128]{1,0:T(8,128)(2,1)} %get-tuple-element.14), channel_id=1, source_target_pairs={{0,4},{1,5},{2,6},{3,7},{4,0},{5,1},{6,2},{7,3},{8,12},{9,13},{10,... | collective-permute-start | bytes 1572872 | tf_op jit(solution)/shard_map/ppermute | solution.py:164
  16.6 2.1 %collective-permute-done.1.refs_1_ = bf16[1536,128]{1,0:T(8,128)(2,1)S(1)} collective-permute-done((bf16[1536,128]{1,0:T(8,128)(2,1)S(1)}, bf16[1536,128]{1,0:T(8,128)(2,1)S(1)}, u32[]{:S(2)}, u32[]{:S(2)}) %collective-permute-start.1) | collective-permute-done | bytes 393248 | tf_op jit(solution)/shard_map/ppermute | solution.py:164
  19.4 5.5 %collective-permute-done.refs_0_ = bf16[1536,128]{1,0:T(8,128)(2,1)} collective-permute-done((bf16[1536,128]{1,0:T(8,128)(2,1)S(1)}, bf16[1536,128]{1,0:T(8,128)(2,1)}, u32[]{:S(2)}, u32[]{:S(2)}) %collective-permute-start) | collective-permute-done | bytes 393248 | tf_op jit(solution)/shard_map/ppermute | solution.py:164
  24.9 2.5 %join.1 = (bf16[3456,128]{1,0:T(8,128)(2,1)S(1)}, bf16[3456,128]{1,0:T(8,128)(2,1)S(1)}, bf16[3456,128]{1,0:T(8,128)(2,1)S(1)}, bf16[3456,128]{1,0:T(8,128)(2,1)S(1)}, bf16[4608,128]{1,0:T(8,128)(2,1)}) custom-call(bf16[1536,128]{1,0:T(8,128)(2,1)} %collective-permute-done.refs_0_, bf16[1536,128]{1,0:T(8,128)(2,1)} %copy-done.9, bf16[1536,128]{1,0:T(8,128)(2,1)} %copy-done.8), custom_call_target="tpu_custom_call" | custom-call | tf_op jit(solution)/shard_map/join/pallas_call | solution.py:215
  28.6 16.8 %collective-permute-done.5 = bf16[2048,128]{1,0:T(8,128)(2,1)} collective-permute-done((bf16[2048,128]{1,0:T(8,128)(2,1)}, bf16[2048,128]{1,0:T(8,128)(2,1)}, u32[]{:S(2)}, u32[]{:S(2)}) %collective-permute-start.5) | collective-permute-done | bytes 524320 | tf_op jit(solution)/shard_map/ppermute | solution.py:164
  45.4 1.7 %collective-permute-start.14 = (bf16[2048,128]{1,0:T(8,128)(2,1)}, bf16[2048,128]{1,0:T(8,128)(2,1)S(1)}, u32[]{:S(2)}, u32[]{:S(2)}) collective-permute-start(bf16[2048,128]{1,0:T(8,128)(2,1)} %collective-permute-done.5), channel_id=1, source_target_pairs={{0,1},{1,0},{2,3},{3,2},{4,5},{5,4},{6,7},{7,6},{8,9},{9,8},{10,11... | collective-permute-start | bytes 1572872 | tf_op jit(solution)/shard_map/ppermute | solution.py:164
  47.0 3.5 %collective-permute-start.13 = (bf16[2048,128]{1,0:T(8,128)(2,1)}, bf16[2048,128]{1,0:T(8,128)(2,1)S(1)}, u32[]{:S(2)}, u32[]{:S(2)}) collective-permute-start(bf16[2048,128]{1,0:T(8,128)(2,1)} %collective-permute-done.4), channel_id=1, source_target_pairs={{0,1},{1,0},{2,3},{3,2},{4,5},{5,4},{6,7},{7,6},{8,9},{9,8},{10,11... | collective-permute-start | bytes 1572872 | tf_op jit(solution)/shard_map/ppermute | solution.py:164
  52.3 2.5 %collective-permute-start.7 = (bf16[3456,128]{1,0:T(8,128)(2,1)S(1)}, bf16[3456,128]{1,0:T(8,128)(2,1)}, u32[]{:S(2)}, u32[]{:S(2)}) collective-permute-start(bf16[3456,128]{1,0:T(8,128)(2,1)S(1)} %get-tuple-element.16), channel_id=1, source_target_pairs={{0,24},{1,25},{2,26},{3,27},{4,28},{5,29},{6,30},{7,31},{8,0},{9,1... | collective-permute-start | bytes 2654216 | tf_op jit(solution)/shard_map/ppermute | solution.py:164
  54.8 1.3 collective-permute-start.8
  56.1 1.5 %collective-permute-start.9 = (bf16[3456,128]{1,0:T(8,128)(2,1)S(1)}, bf16[3456,128]{1,0:T(8,128)(2,1)S(1)}, u32[]{:S(2)}, u32[]{:S(2)}) collective-permute-start(bf16[3456,128]{1,0:T(8,128)(2,1)S(1)} %get-tuple-element.18), channel_id=1, source_target_pairs={{0,96},{1,97},{2,98},{3,99},{4,100},{5,101},{6,102},{7,103},{8,104... | collective-permute-start | bytes 2654216 | tf_op jit(solution)/shard_map/ppermute | solution.py:164
  57.6 15.8 %collective-permute-done.7 = bf16[3456,128]{1,0:T(8,128)(2,1)} collective-permute-done((bf16[3456,128]{1,0:T(8,128)(2,1)S(1)}, bf16[3456,128]{1,0:T(8,128)(2,1)}, u32[]{:S(2)}, u32[]{:S(2)}) %collective-permute-start.7) | collective-permute-done | bytes 884768 | tf_op jit(solution)/shard_map/ppermute | solution.py:164
  73.4 1.2 collective-permute-start.15
  74.7 2.1 %collective-permute-done.8 = bf16[3456,128]{1,0:T(8,128)(2,1)} collective-permute-done((bf16[3456,128]{1,0:T(8,128)(2,1)S(1)}, bf16[3456,128]{1,0:T(8,128)(2,1)}, u32[]{:S(2)}, u32[]{:S(2)}) %collective-permute-start.8) | collective-permute-done | bytes 884768 | tf_op jit(solution)/shard_map/ppermute | solution.py:164
  76.8 1.4 %collective-permute-start.16 = (bf16[3456,128]{1,0:T(8,128)(2,1)}, bf16[3456,128]{1,0:T(8,128)(2,1)S(1)}, u32[]{:S(2)}, u32[]{:S(2)}) collective-permute-start(bf16[3456,128]{1,0:T(8,128)(2,1)} %collective-permute-done.7), channel_id=1, source_target_pairs={{0,1},{1,0},{2,3},{3,2},{4,5},{5,4},{6,7},{7,6},{8,9},{9,8},{10,11... | collective-permute-start | bytes 2654216 | tf_op jit(solution)/shard_map/ppermute | solution.py:164
  78.9 2.3 %local_compaction.1 = s32[128,128]{1,0:T(8,128)} custom-call(s32[32,128]{1,0:T(8,128)} %bitcast.43, s32[32,128]{1,0:T(8,128)} %bitcast.44), custom_call_target="tpu_custom_call" | custom-call | tf_op jit(solution)/shard_map/local_compaction/pallas_call | solution.py:252
  81.2 17.4 %all_to_all.22 = s32[128,1,128]{2,1,0:T(1,128)S(1)} all-to-all(s32[128,1,128]{2,1,0:T(1,128)} %bitcast.42), channel_id=1, replica_groups=mesh['rows'=16,'dict'=8] {'rows','dict'}, dimensions={0} | all-to-all | bytes 131072 | tf_op jit(solution)/shard_map/all_to_all | solution.py:244
  99.9 3.2 %regroup.1 = s32[128,128]{1,0:T(8,128)} custom-call(s32[1]{0:T(128)} %bitcast.me_ref, s32[128]{0:T(128)} %slice_reduce_fusion.counts_ref, s32[128,128]{1,0:T(8,128)} %bitcast.37), custom_call_target="tpu_custom_call" | custom-call | tf_op jit(solution)/shard_map/regroup/pallas_call | solution.py:258
  103.1 14.4 %all_to_all.23 = s32[128,1,128]{2,1,0:T(1,128)S(1)} all-to-all(s32[128,1,128]{2,1,0:T(1,128)} %bitcast.41), channel_id=1, replica_groups=mesh['rows'=16,'dict'=8] {'rows','dict'}, dimensions={0} | all-to-all | bytes 131072 | tf_op jit(solution)/shard_map/all_to_all | solution.py:244
  119.0 12.1 %decode.1 = bf16[4096,128]{1,0:T(8,128)(2,1)} custom-call(s32[1]{0:T(128)} %bitcast.me_ref, s32[128,128]{1,0:T(8,128)S(1)} %bitcast.29, bf16[4096,2,128]{2,1,0:T(2,128)(2,1)} %bitcast.30, bf16[2304,2,128]{2,1,0:T(2,128)(2,1)} %bitcast.31, bf16[1024,2,128]{2,1,0:T(2,128)(2,1)} %bitcast.11.refs_2_, bf16[1024,2,128]{2,1,0:T(2,128)(2,1)} %bitcast.12.refs_3_, ...), custom_call_target="tpu_custom_call" | custom-call | tf_op jit(solution)/shard_map/decode/pallas_call | solution.py:271
  (42 shorter events, 7.3 us)
Async XLA Ops:
  2.1 12.4 %collective-permute-start.2 = (bf16[1536,128]{1,0:T(8,128)(2,1)S(1)}, bf16[1536,128]{1,0:T(8,128)(2,1)S(1)}, u32[]{:S(2)}, u32[]{:S(2)}) collective-permute-start(bf16[1536,128]{1,0:T(8,128)(2,1)S(1)} %get-tuple-element.12), channel_id=1, source_target_pairs={{0,6},{1,7},{2,0},{3,1},{4,2},{5,3},{6,4},{7,5},{8,14},{9,15},{10,... | collective-permute-start | bytes 1179656 | tf_op jit(solution)/shard_map/ppermute | solution.py:164
  6.7 38.7 %collective-permute-start.5 = (bf16[2048,128]{1,0:T(8,128)(2,1)}, bf16[2048,128]{1,0:T(8,128)(2,1)}, u32[]{:S(2)}, u32[]{:S(2)}) collective-permute-start(bf16[2048,128]{1,0:T(8,128)(2,1)} %get-tuple-element.14), channel_id=1, source_target_pairs={{0,6},{1,7},{2,0},{3,1},{4,2},{5,3},{6,4},{7,5},{8,14},{9,15},{10,... | collective-permute-start | bytes 1572872 | tf_op jit(solution)/shard_map/ppermute | solution.py:164
  6.8 11.8 %collective-permute-start.1 = (bf16[1536,128]{1,0:T(8,128)(2,1)S(1)}, bf16[1536,128]{1,0:T(8,128)(2,1)S(1)}, u32[]{:S(2)}, u32[]{:S(2)}) collective-permute-start(bf16[1536,128]{1,0:T(8,128)(2,1)S(1)} %get-tuple-element.12), channel_id=1, source_target_pairs={{0,2},{1,3},{2,4},{3,5},{4,6},{5,7},{6,0},{7,1},{8,10},{9,11},{10,... | collective-permute-start | bytes 1179656 | tf_op jit(solution)/shard_map/ppermute | solution.py:164
  8.2 16.7 %collective-permute-start = (bf16[1536,128]{1,0:T(8,128)(2,1)S(1)}, bf16[1536,128]{1,0:T(8,128)(2,1)}, u32[]{:S(2)}, u32[]{:S(2)}) collective-permute-start(bf16[1536,128]{1,0:T(8,128)(2,1)S(1)} %get-tuple-element.12), channel_id=1, source_target_pairs={{0,4},{1,5},{2,6},{3,7},{4,0},{5,1},{6,2},{7,3},{8,12},{9,13},{10,... | collective-permute-start | bytes 1179656 | tf_op jit(solution)/shard_map/ppermute | solution.py:164
  8.2 38.9 %collective-permute-start.4 = (bf16[2048,128]{1,0:T(8,128)(2,1)}, bf16[2048,128]{1,0:T(8,128)(2,1)}, u32[]{:S(2)}, u32[]{:S(2)}) collective-permute-start(bf16[2048,128]{1,0:T(8,128)(2,1)} %get-tuple-element.14), channel_id=1, source_target_pairs={{0,2},{1,3},{2,4},{3,5},{4,6},{5,7},{6,0},{7,1},{8,10},{9,11},{10,... | collective-permute-start | bytes 1572872 | tf_op jit(solution)/shard_map/ppermute | solution.py:164
  14.5 4.1 %copy-start.8 = (bf16[1536,128]{1,0:T(8,128)(2,1)}, bf16[1536,128]{1,0:T(8,128)(2,1)S(1)}, u32[]{:S(2)}) copy-start(bf16[1536,128]{1,0:T(8,128)(2,1)S(1)} %collective-permute-done.2.refs_2_) | copy-start | bytes 1179652
  14.5 36.1 %collective-permute-start.3 = (bf16[2048,128]{1,0:T(8,128)(2,1)}, bf16[2048,128]{1,0:T(8,128)(2,1)}, u32[]{:S(2)}, u32[]{:S(2)}) collective-permute-start(bf16[2048,128]{1,0:T(8,128)(2,1)} %get-tuple-element.14), channel_id=1, source_target_pairs={{0,4},{1,5},{2,6},{3,7},{4,0},{5,1},{6,2},{7,3},{8,12},{9,13},{10,... | collective-permute-start | bytes 1572872 | tf_op jit(solution)/shard_map/ppermute | solution.py:164
  27.4 28.7 %collective-permute-start.6 = (bf16[3456,128]{1,0:T(8,128)(2,1)S(1)}, bf16[3456,128]{1,0:T(8,128)(2,1)}, u32[]{:S(2)}, u32[]{:S(2)}) collective-permute-start(bf16[3456,128]{1,0:T(8,128)(2,1)S(1)} %get-tuple-element.15), channel_id=1, source_target_pairs={{0,8},{1,9},{2,10},{3,11},{4,12},{5,13},{6,14},{7,15},{8,16},{9,17... | collective-permute-start | bytes 2654216 | tf_op jit(solution)/shard_map/ppermute | solution.py:164
  45.4 5.7 %collective-permute-start.14 = (bf16[2048,128]{1,0:T(8,128)(2,1)}, bf16[2048,128]{1,0:T(8,128)(2,1)S(1)}, u32[]{:S(2)}, u32[]{:S(2)}) collective-permute-start(bf16[2048,128]{1,0:T(8,128)(2,1)} %collective-permute-done.5), channel_id=1, source_target_pairs={{0,1},{1,0},{2,3},{3,2},{4,5},{5,4},{6,7},{7,6},{8,9},{9,8},{10,11... | collective-permute-start | bytes 1572872 | tf_op jit(solution)/shard_map/ppermute | solution.py:164
  47.0 5.3 %collective-permute-start.13 = (bf16[2048,128]{1,0:T(8,128)(2,1)}, bf16[2048,128]{1,0:T(8,128)(2,1)S(1)}, u32[]{:S(2)}, u32[]{:S(2)}) collective-permute-start(bf16[2048,128]{1,0:T(8,128)(2,1)} %collective-permute-done.4), channel_id=1, source_target_pairs={{0,1},{1,0},{2,3},{3,2},{4,5},{5,4},{6,7},{7,6},{8,9},{9,8},{10,11... | collective-permute-start | bytes 1572872 | tf_op jit(solution)/shard_map/ppermute | solution.py:164
  50.6 4.2 %collective-permute-start.12 = (bf16[2048,128]{1,0:T(8,128)(2,1)}, bf16[2048,128]{1,0:T(8,128)(2,1)S(1)}, u32[]{:S(2)}, u32[]{:S(2)}) collective-permute-start(bf16[2048,128]{1,0:T(8,128)(2,1)} %collective-permute-done.3), channel_id=1, source_target_pairs={{0,1},{1,0},{2,3},{3,2},{4,5},{5,4},{6,7},{7,6},{8,9},{9,8},{10,11... | collective-permute-start | bytes 1572872 | tf_op jit(solution)/shard_map/ppermute | solution.py:164
  50.6 66.9 %collective-permute-start.10 = (bf16[8192,128]{1,0:T(8,128)(2,1)}, bf16[8192,128]{1,0:T(8,128)(2,1)}, u32[]{:S(2)}, u32[]{:S(2)}) collective-permute-start(bf16[8192,128]{1,0:T(8,128)(2,1)} %table_ref.1), channel_id=1, source_target_pairs={{0,1},{1,0},{2,3},{3,2},{4,5},{5,4},{6,7},{7,6},{8,9},{9,8},{10,11... | collective-permute-start | bytes 6291464 | tf_op jit(solution)/shard_map/ppermute | solution.py:164
  51.1 27.2 %copy-start.5 = (bf16[2048,128]{1,0:T(8,128)(2,1)}, bf16[2048,128]{1,0:T(8,128)(2,1)S(1)}, u32[]{:S(2)}) copy-start(bf16[2048,128]{1,0:T(8,128)(2,1)S(1)} %collective-permute-done.14) | copy-start | bytes 1572868
  51.1 27.3 %collective-permute-start.11 = (bf16[4608,128]{1,0:T(8,128)(2,1)}, bf16[4608,128]{1,0:T(8,128)(2,1)}, u32[]{:S(2)}, u32[]{:S(2)}) collective-permute-start(bf16[4608,128]{1,0:T(8,128)(2,1)} %get-tuple-element.13), channel_id=1, source_target_pairs={{0,1},{1,0},{2,3},{3,2},{4,5},{5,4},{6,7},{7,6},{8,9},{9,8},{10,11... | collective-permute-start | bytes 3538952 | tf_op jit(solution)/shard_map/ppermute | solution.py:164
  52.3 26.0 %copy-start.6 = (bf16[2048,128]{1,0:T(8,128)(2,1)}, bf16[2048,128]{1,0:T(8,128)(2,1)S(1)}, u32[]{:S(2)}) copy-start(bf16[2048,128]{1,0:T(8,128)(2,1)S(1)} %collective-permute-done.13) | copy-start | bytes 1572868
  52.3 21.1 %collective-permute-start.7 = (bf16[3456,128]{1,0:T(8,128)(2,1)S(1)}, bf16[3456,128]{1,0:T(8,128)(2,1)}, u32[]{:S(2)}, u32[]{:S(2)}) collective-permute-start(bf16[3456,128]{1,0:T(8,128)(2,1)S(1)} %get-tuple-element.16), channel_id=1, source_target_pairs={{0,24},{1,25},{2,26},{3,27},{4,28},{5,29},{6,30},{7,31},{8,0},{9,1... | collective-permute-start | bytes 2654216 | tf_op jit(solution)/shard_map/ppermute | solution.py:164
  54.8 24.1 %copy-start.7 = (bf16[2048,128]{1,0:T(8,128)(2,1)}, bf16[2048,128]{1,0:T(8,128)(2,1)S(1)}, u32[]{:S(2)}) copy-start(bf16[2048,128]{1,0:T(8,128)(2,1)S(1)} %collective-permute-done.12) | copy-start | bytes 1572868
  54.8 22.0 %collective-permute-start.8 = (bf16[3456,128]{1,0:T(8,128)(2,1)S(1)}, bf16[3456,128]{1,0:T(8,128)(2,1)}, u32[]{:S(2)}, u32[]{:S(2)}) collective-permute-start(bf16[3456,128]{1,0:T(8,128)(2,1)S(1)} %get-tuple-element.17), channel_id=1, source_target_pairs={{0,32},{1,33},{2,34},{3,35},{4,36},{5,37},{6,38},{7,39},{8,40},{9,... | collective-permute-start | bytes 2654216 | tf_op jit(solution)/shard_map/ppermute | solution.py:164
  56.1 22.1 %collective-permute-start.9 = (bf16[3456,128]{1,0:T(8,128)(2,1)S(1)}, bf16[3456,128]{1,0:T(8,128)(2,1)S(1)}, u32[]{:S(2)}, u32[]{:S(2)}) collective-permute-start(bf16[3456,128]{1,0:T(8,128)(2,1)S(1)} %get-tuple-element.18), channel_id=1, source_target_pairs={{0,96},{1,97},{2,98},{3,99},{4,100},{5,101},{6,102},{7,103},{8,104... | collective-permute-start | bytes 2654216 | tf_op jit(solution)/shard_map/ppermute | solution.py:164
  73.4 44.0 %collective-permute-start.15 = (bf16[3456,128]{1,0:T(8,128)(2,1)}, bf16[3456,128]{1,0:T(8,128)(2,1)S(1)}, u32[]{:S(2)}, u32[]{:S(2)}) collective-permute-start(bf16[3456,128]{1,0:T(8,128)(2,1)} %collective-permute-done.6), channel_id=1, source_target_pairs={{0,1},{1,0},{2,3},{3,2},{4,5},{5,4},{6,7},{7,6},{8,9},{9,8},{10,11... | collective-permute-start | bytes 2654216 | tf_op jit(solution)/shard_map/ppermute | solution.py:164
  76.8 40.7 %collective-permute-start.16 = (bf16[3456,128]{1,0:T(8,128)(2,1)}, bf16[3456,128]{1,0:T(8,128)(2,1)S(1)}, u32[]{:S(2)}, u32[]{:S(2)}) collective-permute-start(bf16[3456,128]{1,0:T(8,128)(2,1)} %collective-permute-done.7), channel_id=1, source_target_pairs={{0,1},{1,0},{2,3},{3,2},{4,5},{5,4},{6,7},{7,6},{8,9},{9,8},{10,11... | collective-permute-start | bytes 2654216 | tf_op jit(solution)/shard_map/ppermute | solution.py:164
  78.3 39.3 %copy-start = (bf16[3456,128]{1,0:T(8,128)(2,1)}, bf16[3456,128]{1,0:T(8,128)(2,1)S(1)}, u32[]{:S(2)}) copy-start(bf16[3456,128]{1,0:T(8,128)(2,1)S(1)} %collective-permute-done.9) | copy-start | bytes 2654212
  78.3 39.2 %collective-permute-start.17 = (bf16[3456,128]{1,0:T(8,128)(2,1)}, bf16[3456,128]{1,0:T(8,128)(2,1)S(1)}, u32[]{:S(2)}, u32[]{:S(2)}) collective-permute-start(bf16[3456,128]{1,0:T(8,128)(2,1)} %collective-permute-done.8), channel_id=1, source_target_pairs={{0,1},{1,0},{2,3},{3,2},{4,5},{5,4},{6,7},{7,6},{8,9},{9,8},{10,11... | collective-permute-start | bytes 2654216 | tf_op jit(solution)/shard_map/ppermute | solution.py:164
  78.4 39.2 %collective-permute-start.18 = (bf16[3456,128]{1,0:T(8,128)(2,1)S(1)}, bf16[3456,128]{1,0:T(8,128)(2,1)}, u32[]{:S(2)}, u32[]{:S(2)}) collective-permute-start(bf16[3456,128]{1,0:T(8,128)(2,1)S(1)} %collective-permute-done.9), channel_id=1, source_target_pairs={{0,1},{1,0},{2,3},{3,2},{4,5},{5,4},{6,7},{7,6},{8,9},{9,8},{10,11... | collective-permute-start | bytes 2654216 | tf_op jit(solution)/shard_map/ppermute | solution.py:164
  (5 other events, 5.0 us)

commit v3 on v2

--- a/solution.py
+++ b/solution.py
@@ -8,15 +8,16 @@
 
 ALL = ("rows", "dict")
 LANES = 128
-PRESENT = 1 << 30
+PRESENT = 1 << 23
 DEVICES = 128
 BLOCKS = 32
 SHARD = 8192
-PART = 768
-HALF = PART // 2
-REST = SHARD - 8 * PART
+RING = (2, -1, 1)
+LARGE, SMALLER = (1216, 672, 672), (832, 480, 480)
+BOTH = tuple(large + smaller for large, smaller in zip(LARGE, SMALLER))
+REST = SHARD - 4 * BOTH[1]
 ENTRIES = 8 * SHARD
-RING = (2, -1, 1)
+SMALL = pltpu.CompilerParams(vmem_limit_bytes=8 << 20)
 
 
 def iota(shape, dim):
@@ -39,7 +40,7 @@
     count = jnp.sum(row_sums, axis=0, keepdims=True).astype(jnp.int32)
     here = iota((rows, LANES), 0) * LANES + iota((rows, LANES), 1)
     lane = iota((rows, LANES), 1)
-    item = jnp.where(flags > 0, PRESENT | ((here - position) << 16) | keys_ref[...], 0)
+    item = jnp.where(flags > 0, ((here - position) << 16) | keys_ref[...], 0)
     for level in range((rows * LANES - 1).bit_length()):
         step = 1 << level
         moving = (item >> (16 + level)) & 1 == 1
@@ -55,7 +56,7 @@
     out_ref[...] = jnp.concatenate([codes, counts], axis=0).T
 
 
-def regroup(me_ref, counts_ref, got_ref, out_ref, low_ref, high_ref, rows_ref):
+def regroup(me_ref, got_ref, out_ref):
     me = me_ref[0]
     got = got_ref[...]
     shape = got.shape
@@ -73,18 +74,17 @@
     odd = iota(shape, 0) & 1 == 1
     low = jnp.where(lane < BLOCKS, item, 0)
     high = jnp.where(lane < BLOCKS, pltpu.roll(item, LANES - BLOCKS, 1), 0)
-    low_ref[...] = jnp.where(odd, pltpu.roll(low, BLOCKS, 1), low)
-    high_ref[...] = jnp.where(odd, pltpu.roll(high, BLOCKS, 1), high)
-    rows_ref[...] = jnp.zeros_like(rows_ref)
-
-    def place(s, before):
-        d = (before + me) >> 12
-        rows_ref[pl.ds(d, 1), :] = rows_ref[pl.ds(d, 1), :] | low_ref[pl.ds(s, 1), :]
-        rows_ref[pl.ds(d + 1, 1), :] = rows_ref[pl.ds(d + 1, 1), :] | high_ref[pl.ds(s, 1), :]
-        return before + counts_ref[s]
-
-    lax.fori_loop(0, DEVICES, place, jnp.int32(0), unroll=8)
-    out_ref[...] = rows_ref[:DEVICES, :]
+    low = jnp.where(odd, pltpu.roll(low, BLOCKS, 1), low)
+    high = jnp.where(odd, pltpu.roll(high, BLOCKS, 1), high)
+    both = jnp.concatenate([low, high], axis=0)
+    device = (start >> 12).T
+    here = iota(shape, 0)
+    chosen = [jnp.where(device + next_one == here, 1.0, 0.0) for next_one in (0, 1)]
+    chosen = jnp.concatenate(chosen, axis=1)
+    total = exact_dot(chosen, (both & 255).astype(jnp.float32))
+    total += 256 * exact_dot(chosen, ((both >> 8) & 255).astype(jnp.float32))
+    total += 65536 * exact_dot(chosen, (both >> 16).astype(jnp.float32))
+    out_ref[...] = total.astype(jnp.int32)
 
 
 def colours(x, y):
@@ -95,22 +95,21 @@
     x, y, z, core = (me >> 3) & 3, me >> 5, (me >> 1) & 3, (me & 1) ^ half
     a, b = colours(x, y)
     bases = [(((z + step) & 3) * 2 + core) * SHARD for step in RING]
-
-    def first(colour, at=0):
-        return PART * (colour & 3) + at
-
-    def second(colour, at=0):
-        return PART * (4 + (colour & 3)) + at
-
-    def pieces(whole, part):
-        return [(PART, base + whole) for base in bases] + [(HALF, base + part) for base in bases]
-
-    parts = [[(SHARD, (z * 2 + core) * SHARD)]]
-    parts += [[(PART, base + at) for base in bases for at in (first(a), second(b))]]
-    parts += [[(REST, base + 8 * PART)] for base in bases]
-    parts += [pieces(first(a - 1), second(b + 2)), pieces(first(a + 1), second(b + 2, HALF))]
-    parts += [pieces(second(b - 1), first(a + 2)), pieces(second(b + 1), first(a + 2, HALF))]
-    return parts
+    a_rows = list(zip(LARGE, bases))
+    b_rows = list(zip(SMALLER, [base + 4 * rows for rows, base in a_rows]))
+
+    def whole(parts, colour):
+        return [(rows, base + rows * (colour & 3)) for rows, base in parts]
+
+    def part(parts, colour, at):
+        return [(rows // 2, base + rows * (colour & 3) + at * (rows // 2)) for rows, base in parts]
+
+    places = [[(SHARD, (z * 2 + core) * SHARD)]]
+    places += [[place for pair in zip(whole(a_rows, a), whole(b_rows, b)) for place in pair]]
+    places += [[(REST, base + SHARD - REST)] for base in bases[1:]]
+    places += [whole(a_rows, a - 1) + part(b_rows, b + 2, 0), whole(a_rows, a + 1) + part(b_rows, b + 2, 1)]
+    places += [whole(b_rows, b - 1) + part(a_rows, a + 2, 0), whole(b_rows, b + 1) + part(a_rows, a + 2, 1)]
+    return places
 
 
 def decode(me_ref, got_ref, *refs):
@@ -164,21 +163,24 @@
     return lax.ppermute(x, ALL, pairs)
 
 
-def along_z(piece):
-    return [moved(piece, lambda x, y, z, core, step=step: (x, y, z - step, core)) for step in RING]
+def along_z(pieces, steps):
+    return [
+        moved(piece, lambda x, y, z, core, step=step: (x, y, z - step, core)) for piece, step in zip(pieces, steps)
+    ]
 
 
 def other_core(piece):
     return moved(piece, lambda x, y, z, core: (x, y, z, 1 - core))
 
 
-def cut(me_ref, table_ref, parts_ref, rest_ref, sems):
+def cut(me_ref, table_ref, far_ref, near_ref, sems):
     a, b = colours((me_ref[0] >> 3) & 3, me_ref[0] >> 5)
-    copies = [
-        pltpu.make_async_copy(table_ref.at[pl.ds(PART * a, PART)], parts_ref.at[pl.ds(0, PART)], sems.at[0]),
-        pltpu.make_async_copy(table_ref.at[pl.ds(PART * (4 + b), PART)], parts_ref.at[pl.ds(PART, PART)], sems.at[1]),
-        pltpu.make_async_copy(table_ref.at[pl.ds(8 * PART, REST)], rest_ref, sems.at[2]),
-    ]
+    copies = []
+    for out, large, smaller in ((far_ref, LARGE[0], SMALLER[0]), (near_ref, LARGE[1], SMALLER[1])):
+        for at, to, rows in ((large * a, 0, large), (4 * large + smaller * b, large, smaller)):
+            copies.append(
+                pltpu.make_async_copy(table_ref.at[pl.ds(at, rows)], out.at[pl.ds(to, rows)], sems.at[len(copies)])
+            )
     for copy in copies:
         copy.start()
     for copy in copies:
@@ -187,45 +189,55 @@
 
 def join(*refs):
     pieces, joined, all_ref = refs[: len(RING)], refs[len(RING) : -1], refs[-1]
-    for out, (whole, part) in zip(joined, ((0, PART), (0, PART + HALF), (PART, 0), (PART, HALF))):
-        for k, piece in enumerate(pieces):
-            out[PART * k : PART * (k + 1), :] = piece[whole : whole + PART, :]
-            to = PART * len(RING) + HALF * k
-            out[to : to + HALF, :] = piece[part : part + HALF, :]
-    for k, piece in enumerate(pieces):
-        all_ref[2 * PART * k : 2 * PART * (k + 1), :] = piece[...]
+    for number, out in enumerate(joined):
+        to = 0
+        for share in (1, 2):
+            for large, smaller, piece in zip(LARGE, SMALLER, pieces):
+                begin, rows = (0, large) if (number < 2) == (share == 1) else (large, smaller)
+                rows //= share
+                begin += rows * (number % 2) * (share - 1)
+                out[to : to + rows, :] = piece[begin : begin + rows, :]
+                to += rows
+    to = 0
+    for rows, piece in zip(BOTH, pieces):
+        all_ref[to : to + rows, :] = piece[...]
+        to += rows
 
 
 def first_pieces(me, table):
-    parts, rest = pl.pallas_call(
+    far, near = pl.pallas_call(
         cut,
-        out_shape=[pltpu.VMEM((rows, LANES), table.dtype) for rows in (2 * PART, REST)],
+        out_shape=[pltpu.VMEM((rows, LANES), table.dtype) for rows in BOTH[:2]],
         in_specs=[smem(), anywhere()],
         out_specs=[vmem()] * 2,
-        scratch_shapes=[pltpu.SemaphoreType.DMA((3,))],
+        scratch_shapes=[pltpu.SemaphoreType.DMA((4,))],
         name="cut",
-    )(me, table)
-    first = along_z(parts)
-    rest = along_z(rest)
+    )(me, pltpu.with_memory_space_constraint(table, pltpu.HBM))
+    first = along_z([far, near, near], RING)
+    rest = along_z([table[SHARD - REST :]] * 2, RING[1:])
     return first, rest
 
 
 def ring_pieces(first):
-    rows = len(RING) * (PART + HALF)
+    rows = [sum(LARGE) + sum(SMALLER) // 2] * 2 + [sum(SMALLER) + sum(LARGE) // 2] * 2
     *sent, every = pl.pallas_call(
         join,
-        out_shape=[pltpu.VMEM((rows, LANES), first[0].dtype)] * 4
-        + [jax.ShapeDtypeStruct((2 * PART * len(RING), LANES), first[0].dtype)],
+        out_shape=[pltpu.VMEM((count, LANES), first[0].dtype) for count in rows]
+        + [jax.ShapeDtypeStruct((sum(BOTH), LANES), first[0].dtype)],
         in_specs=[vmem()] * len(first),
         out_specs=[vmem()] * 5,
+        compiler_params=SMALL,
         name="join",
     )(*first)
-    return every, [
+    ring = [
         moved(sent[0], lambda x, y, z, core: (x + 1, y, z, core)),
         moved(sent[1], lambda x, y, z, core: (x - 1, y, z, core)),
+    ]
+    ring += [
         moved(sent[2], lambda x, y, z, core: (x, y + 1, z, core)),
         moved(sent[3], lambda x, y, z, core: (x, y - 1, z, core)),
     ]
+    return every, ring
 
 
 def anywhere():
@@ -249,7 +261,7 @@
     square = jax.ShapeDtypeStruct((DEVICES, LANES), jnp.int32)
     first, rest = first_pieces(me, decoding_table)
     other_table = other_core(decoding_table)
-    sent = pl.pallas_call(local_compaction, out_shape=square, in_specs=[vmem(), vmem()], out_specs=vmem(), name="local_compaction")(
+    sent = pl.pallas_call(local_compaction, out_shape=square, in_specs=[vmem(), vmem()], out_specs=vmem(), compiler_params=SMALL, name="local_compaction")(
         lookup_keys_per_record.reshape(BLOCKS, LANES), filter_passed_flags.reshape(BLOCKS, LANES)
     )
     got = exchange(sent)
@@ -258,14 +270,15 @@
     sent = pl.pallas_call(
         regroup,
         out_shape=square,
-        in_specs=[smem(), smem(), vmem()],
+        in_specs=[smem(), vmem()],
         out_specs=vmem(),
-        scratch_shapes=[pltpu.VMEM((DEVICES, LANES), jnp.int32)] * 2 + [pltpu.VMEM((DEVICES + 8, LANES), jnp.int32)],
+        compiler_params=SMALL,
         name="regroup",
-    )(me, got[:, BLOCKS], got)
+    )(me, got)
     got = exchange(sent)
     other_rest = [other_core(piece) for piece in rest]
-    other_ring = [other_core(piece) for piece in ring]
+    other_ring = [other_core(piece) for piece in ring[:2]]
+    other_ring += [other_core(piece) for piece in ring[2:]]
     pieces = [decoding_table, every, *rest, *ring, other_table, other_every, *other_rest, *other_ring]
     pieces = [pltpu.with_memory_space_constraint(piece.reshape(-1, 2, LANES), pltpu.HBM) for piece in pieces]
     return pl.pallas_call(

time: 131 us -> 136 us (1.038)
  the two profiles are of different devices: /device:TPU:1 before, /device:TPU:4 now
where the time goes in v3:
time: 136 us; the launch traced here: 134 us
  waiting for transfers between devices  68.8 us (51%)
  blocking collectives  31.3 us (23%)
  Pallas kernels  15.7 us (12%)
  starting transfers between devices  15.4 us (11%)
  local copies, waits for them, and re-layouts  2.3 us (2%)
    ppermute x17, waiting for transfers between devices, moved(): return lax.ppermute(x, ALL, pairs)  68.8 us
    all_to_all x2, blocking collectives, exchange(): return lax.all_to_all(x, ALL, 0, 0, tiled=True)  31.3 us
    ppermute x17, starting transfers between devices, moved(): return lax.ppermute(x, ALL, pairs)  15.4 us
    pallas_call x1, Pallas kernels, steps(): pl.pallas_call(decode, out_shape=jax.ShapeDtypeStruct((BLOCKS * LANES, LA...  12 us
  transfers between devices with their start and end apart: 17, of which 3 were waited for; matrix products, arithmetic and copies ran while one was open for 0% of the time, Pallas kernels for 2%

profile of v3, /device:TPU:4, one launch (start us, length us, event | category | flops | bytes accessed | tf_op | source)
XLA Modules:
  0.0 133.7 jit_solution(6032572018714009662)
XLA Ops:
  0.0 1.3 cut.1
  1.4 4.0 %collective-permute-start = (bf16[2048,128]{1,0:T(8,128)(2,1)S(1)}, bf16[2048,128]{1,0:T(8,128)(2,1)S(1)}, u32[]{:S(2)}, u32[]{:S(2)}) collective-permute-start(bf16[2048,128]{1,0:T(8,128)(2,1)S(1)} %get-tuple-element.12), channel_id=1, source_target_pairs={{0,4},{1,5},{2,6},{3,7},{4,0},{5,1},{6,2},{7,3},{8,12},{9,13},{10,... | collective-permute-start | bytes 1572872 | tf_op jit(solution)/shard_map/ppermute | solution.py:163
  5.4 0.8 collective-permute-start.4
  6.2 1.3 collective-permute-start.3
  7.5 1.9 %collective-permute-start.2 = (bf16[1152,128]{1,0:T(8,128)(2,1)S(1)}, bf16[1152,128]{1,0:T(8,128)(2,1)S(1)}, u32[]{:S(2)}, u32[]{:S(2)}) collective-permute-start(bf16[1152,128]{1,0:T(8,128)(2,1)S(1)} %get-tuple-element.13), channel_id=1, source_target_pairs={{0,6},{1,7},{2,0},{3,1},{4,2},{5,3},{6,4},{7,5},{8,14},{9,15},{10,... | collective-permute-start | bytes 884744 | tf_op jit(solution)/shard_map/ppermute | solution.py:163
  9.5 34.5 %collective-permute-done.2.refs_2_ = bf16[1152,128]{1,0:T(8,128)(2,1)S(1)} collective-permute-done((bf16[1152,128]{1,0:T(8,128)(2,1)S(1)}, bf16[1152,128]{1,0:T(8,128)(2,1)S(1)}, u32[]{:S(2)}, u32[]{:S(2)}) %collective-permute-start.2) | collective-permute-done | bytes 294944 | tf_op jit(solution)/shard_map/ppermute | solution.py:163
  44.0 0.3 join.1
  44.4 1.3 collective-permute-start.5
  45.6 1.6 %collective-permute-start.7 = (bf16[3072,128]{1,0:T(8,128)(2,1)S(1)}, bf16[3072,128]{1,0:T(8,128)(2,1)S(1)}, u32[]{:S(2)}, u32[]{:S(2)}) collective-permute-start(bf16[3072,128]{1,0:T(8,128)(2,1)S(1)} %get-tuple-element.17), channel_id=1, source_target_pairs={{0,32},{1,33},{2,34},{3,35},{4,36},{5,37},{6,38},{7,39},{8,40},{9,... | collective-permute-start | bytes 2359304 | tf_op jit(solution)/shard_map/ppermute | solution.py:163
  47.2 1.7 %collective-permute-start.8 = (bf16[3072,128]{1,0:T(8,128)(2,1)S(1)}, bf16[3072,128]{1,0:T(8,128)(2,1)S(1)}, u32[]{:S(2)}, u32[]{:S(2)}) collective-permute-start(bf16[3072,128]{1,0:T(8,128)(2,1)S(1)} %get-tuple-element.18), channel_id=1, source_target_pairs={{0,96},{1,97},{2,98},{3,99},{4,100},{5,101},{6,102},{7,103},{8,104... | collective-permute-start | bytes 2359304 | tf_op jit(solution)/shard_map/ppermute | solution.py:163
  48.9 0.5 collective-permute-start.10
  49.4 15.9 %collective-permute-done.7 = bf16[3072,128]{1,0:T(8,128)(2,1)S(1)} collective-permute-done((bf16[3072,128]{1,0:T(8,128)(2,1)S(1)}, bf16[3072,128]{1,0:T(8,128)(2,1)S(1)}, u32[]{:S(2)}, u32[]{:S(2)}) %collective-permute-start.7) | collective-permute-done | bytes 786464 | tf_op jit(solution)/shard_map/ppermute | solution.py:163
  65.3 0.8 collective-permute-start.6
  66.2 0.5 collective-permute-start.11
  66.6 18.4 %collective-permute-done.6 = bf16[3456,128]{1,0:T(8,128)(2,1)S(1)} collective-permute-done((bf16[3456,128]{1,0:T(8,128)(2,1)S(1)}, bf16[3456,128]{1,0:T(8,128)(2,1)S(1)}, u32[]{:S(2)}, u32[]{:S(2)}) %collective-permute-start.6) | collective-permute-done | bytes 884768 | tf_op jit(solution)/shard_map/ppermute | solution.py:163
  85.0 0.5 collective-permute-start.14
  85.6 0.4 collective-permute-start.16
  86.1 0.9 local_compaction.1
  87.0 17.4 %all_to_all.22 = s32[128,1,128]{2,1,0:T(1,128)S(1)} all-to-all(s32[128,1,128]{2,1,0:T(1,128)S(1)} %bitcast.30), channel_id=1, replica_groups=mesh['rows'=16,'dict'=8] {'rows','dict'}, dimensions={0} | all-to-all | bytes 131072 | tf_op jit(solution)/shard_map/all_to_all | solution.py:256
  104.4 1.0 regroup.1
  105.4 13.9 %all_to_all.23 = s32[128,1,128]{2,1,0:T(1,128)S(1)} all-to-all(s32[128,1,128]{2,1,0:T(1,128)S(1)} %bitcast.29), channel_id=1, replica_groups=mesh['rows'=16,'dict'=8] {'rows','dict'}, dimensions={0} | all-to-all | bytes 131072 | tf_op jit(solution)/shard_map/all_to_all | solution.py:256
  119.5 1.2 copy-done.4
  121.4 0.3 copy-done.13
  121.7 12.0 %decode.1 = bf16[4096,128]{1,0:T(8,128)(2,1)} custom-call(s32[1]{0:T(128)} %bitcast.me_ref, s32[128,128]{1,0:T(8,128)S(1)} %bitcast.31, bf16[4096,2,128]{2,1,0:T(2,128)(2,1)} %bitcast.34, bf16[2176,2,128]{2,1,0:T(2,128)(2,1)} %bitcast.27, bf16[1792,2,128]{2,1,0:T(2,128)(2,1)} %bitcast.38, bf16[1792,2,128]{2,1,0:T(2,128)(2,1)} %bitcast.37, ...), custom_call_target="tpu_custom_call" | custom-call | tf_op jit(solution)/shard_map/decode/pallas_call | solution.py:284
  (54 shorter events, 1.1 us)
Async XLA Ops:
  0.0 86.1 %copy-start.1 = (s32[4096]{0:T(1024)S(1)}, s32[4096]{0:T(1024)}, u32[]{:S(2)}) copy-start(s32[4096]{0:T(1024)} %param.3) | copy-start | bytes 49156
  0.0 86.1 %copy-start.2 = (s32[4096]{0:T(1024)S(1)}, s32[4096]{0:T(1024)}, u32[]{:S(2)}) copy-start(s32[4096]{0:T(1024)} %param.4) | copy-start | bytes 49156
  1.4 42.6 %collective-permute-start = (bf16[2048,128]{1,0:T(8,128)(2,1)S(1)}, bf16[2048,128]{1,0:T(8,128)(2,1)S(1)}, u32[]{:S(2)}, u32[]{:S(2)}) collective-permute-start(bf16[2048,128]{1,0:T(8,128)(2,1)S(1)} %get-tuple-element.12), channel_id=1, source_target_pairs={{0,4},{1,5},{2,6},{3,7},{4,0},{5,1},{6,2},{7,3},{8,12},{9,13},{10,... | collective-permute-start | bytes 1572872 | tf_op jit(solution)/shard_map/ppermute | solution.py:163
  5.4 43.5 %collective-permute-start.4 = (bf16[3584,128]{1,0:T(8,128)(2,1)S(1)}, bf16[3584,128]{1,0:T(8,128)(2,1)S(1)}, u32[]{:S(2)}, u32[]{:S(2)}) collective-permute-start(bf16[3584,128]{1,0:T(8,128)(2,1)S(1)} %slice.3), channel_id=1, source_target_pairs={{0,6},{1,7},{2,0},{3,1},{4,2},{5,3},{6,4},{7,5},{8,14},{9,15},{10,... | collective-permute-start | bytes 2752520 | tf_op jit(solution)/shard_map/ppermute | solution.py:163
  6.2 42.7 %collective-permute-start.3 = (bf16[3584,128]{1,0:T(8,128)(2,1)S(1)}, bf16[3584,128]{1,0:T(8,128)(2,1)S(1)}, u32[]{:S(2)}, u32[]{:S(2)}) collective-permute-start(bf16[3584,128]{1,0:T(8,128)(2,1)S(1)} %slice.3), channel_id=1, source_target_pairs={{0,2},{1,3},{2,4},{3,5},{4,6},{5,7},{6,0},{7,1},{8,10},{9,11},{10,... | collective-permute-start | bytes 2752520 | tf_op jit(solution)/shard_map/ppermute | solution.py:163
  7.5 36.5 %collective-permute-start.2 = (bf16[1152,128]{1,0:T(8,128)(2,1)S(1)}, bf16[1152,128]{1,0:T(8,128)(2,1)S(1)}, u32[]{:S(2)}, u32[]{:S(2)}) collective-permute-start(bf16[1152,128]{1,0:T(8,128)(2,1)S(1)} %get-tuple-element.13), channel_id=1, source_target_pairs={{0,6},{1,7},{2,0},{3,1},{4,2},{5,3},{6,4},{7,5},{8,14},{9,15},{10,... | collective-permute-start | bytes 884744 | tf_op jit(solution)/shard_map/ppermute | solution.py:163
  9.4 34.6 %collective-permute-start.1 = (bf16[1152,128]{1,0:T(8,128)(2,1)S(1)}, bf16[1152,128]{1,0:T(8,128)(2,1)S(1)}, u32[]{:S(2)}, u32[]{:S(2)}) collective-permute-start(bf16[1152,128]{1,0:T(8,128)(2,1)S(1)} %get-tuple-element.13), channel_id=1, source_target_pairs={{0,2},{1,3},{2,4},{3,5},{4,6},{5,7},{6,0},{7,1},{8,10},{9,11},{10,... | collective-permute-start | bytes 884744 | tf_op jit(solution)/shard_map/ppermute | solution.py:163
  44.3 75.0 %copy-start = (bf16[4352,128]{1,0:T(8,128)(2,1)}, bf16[4352,128]{1,0:T(8,128)(2,1)S(1)}, u32[]{:S(2)}) copy-start(bf16[4352,128]{1,0:T(8,128)(2,1)S(1)} %get-tuple-element.14) | copy-start | bytes 3342340
  44.4 21.8 %collective-permute-start.5 = (bf16[3456,128]{1,0:T(8,128)(2,1)S(1)}, bf16[3456,128]{1,0:T(8,128)(2,1)S(1)}, u32[]{:S(2)}, u32[]{:S(2)}) collective-permute-start(bf16[3456,128]{1,0:T(8,128)(2,1)S(1)} %get-tuple-element.15), channel_id=1, source_target_pairs={{0,8},{1,9},{2,10},{3,11},{4,12},{5,13},{6,14},{7,15},{8,16},{9,17... | collective-permute-start | bytes 2654216 | tf_op jit(solution)/shard_map/ppermute | solution.py:163
  45.6 19.7 %collective-permute-start.7 = (bf16[3072,128]{1,0:T(8,128)(2,1)S(1)}, bf16[3072,128]{1,0:T(8,128)(2,1)S(1)}, u32[]{:S(2)}, u32[]{:S(2)}) collective-permute-start(bf16[3072,128]{1,0:T(8,128)(2,1)S(1)} %get-tuple-element.17), channel_id=1, source_target_pairs={{0,32},{1,33},{2,34},{3,35},{4,36},{5,37},{6,38},{7,39},{8,40},{9,... | collective-permute-start | bytes 2359304 | tf_op jit(solution)/shard_map/ppermute | solution.py:163
  47.2 18.9 %collective-permute-start.8 = (bf16[3072,128]{1,0:T(8,128)(2,1)S(1)}, bf16[3072,128]{1,0:T(8,128)(2,1)S(1)}, u32[]{:S(2)}, u32[]{:S(2)}) collective-permute-start(bf16[3072,128]{1,0:T(8,128)(2,1)S(1)} %get-tuple-element.18), channel_id=1, source_target_pairs={{0,96},{1,97},{2,98},{3,99},{4,100},{5,101},{6,102},{7,103},{8,104... | collective-permute-start | bytes 2359304 | tf_op jit(solution)/shard_map/ppermute | solution.py:163
  48.9 70.5 %copy-start.6 = (bf16[3584,128]{1,0:T(8,128)(2,1)}, bf16[3584,128]{1,0:T(8,128)(2,1)S(1)}, u32[]{:S(2)}) copy-start(bf16[3584,128]{1,0:T(8,128)(2,1)S(1)} %collective-permute-done.4) | copy-start | bytes 2752516
  48.9 70.4 %collective-permute-start.9 = (bf16[8192,128]{1,0:T(8,128)(2,1)S(1)}, bf16[8192,128]{1,0:T(8,128)(2,1)S(1)}, u32[]{:S(2)}, u32[]{:S(2)}) collective-permute-start(bf16[8192,128]{1,0:T(8,128)(2,1)S(1)} %copy-done.3), channel_id=1, source_target_pairs={{0,1},{1,0},{2,3},{3,2},{4,5},{5,4},{6,7},{7,6},{8,9},{9,8},{10,11... | collective-permute-start | bytes 6291464 | tf_op jit(solution)/shard_map/ppermute | solution.py:163
  48.9 70.5 %copy-start.7 = (bf16[3584,128]{1,0:T(8,128)(2,1)}, bf16[3584,128]{1,0:T(8,128)(2,1)S(1)}, u32[]{:S(2)}) copy-start(bf16[3584,128]{1,0:T(8,128)(2,1)S(1)} %collective-permute-done.3) | copy-start | bytes 2752516
  48.9 36.1 %collective-permute-start.10 = (bf16[4352,128]{1,0:T(8,128)(2,1)S(1)}, bf16[4352,128]{1,0:T(8,128)(2,1)S(1)}, u32[]{:S(2)}, u32[]{:S(2)}) collective-permute-start(bf16[4352,128]{1,0:T(8,128)(2,1)S(1)} %get-tuple-element.14), channel_id=1, source_target_pairs={{0,1},{1,0},{2,3},{3,2},{4,5},{5,4},{6,7},{7,6},{8,9},{9,8},{10,11... | collective-permute-start | bytes 3342344 | tf_op jit(solution)/shard_map/ppermute | solution.py:163
  65.3 54.1 %copy-start.14 = (bf16[3072,128]{1,0:T(8,128)(2,1)}, bf16[3072,128]{1,0:T(8,128)(2,1)S(1)}, u32[]{:S(2)}) copy-start(bf16[3072,128]{1,0:T(8,128)(2,1)S(1)} %collective-permute-done.7) | copy-start | bytes 2359300
  65.3 19.7 %collective-permute-start.6 = (bf16[3456,128]{1,0:T(8,128)(2,1)S(1)}, bf16[3456,128]{1,0:T(8,128)(2,1)S(1)}, u32[]{:S(2)}, u32[]{:S(2)}) collective-permute-start(bf16[3456,128]{1,0:T(8,128)(2,1)S(1)} %get-tuple-element.16), channel_id=1, source_target_pairs={{0,24},{1,25},{2,26},{3,27},{4,28},{5,29},{6,30},{7,31},{8,0},{9,1... | collective-permute-start | bytes 2654216 | tf_op jit(solution)/shard_map/ppermute | solution.py:163
  66.1 53.3 %copy-start.15 = (bf16[3072,128]{1,0:T(8,128)(2,1)}, bf16[3072,128]{1,0:T(8,128)(2,1)S(1)}, u32[]{:S(2)}) copy-start(bf16[3072,128]{1,0:T(8,128)(2,1)S(1)} %collective-permute-done.8) | copy-start | bytes 2359300
  66.1 19.4 %collective-permute-start.12 = (bf16[3584,128]{1,0:T(8,128)(2,1)S(1)}, bf16[3584,128]{1,0:T(8,128)(2,1)S(1)}, u32[]{:S(2)}, u32[]{:S(2)}) collective-permute-start(bf16[3584,128]{1,0:T(8,128)(2,1)S(1)} %collective-permute-done.4), channel_id=1, source_target_pairs={{0,1},{1,0},{2,3},{3,2},{4,5},{5,4},{6,7},{7,6},{8,9},{9,8},{10,11... | collective-permute-start | bytes 2752520 | tf_op jit(solution)/shard_map/ppermute | solution.py:163
  66.2 19.5 %collective-permute-start.11 = (bf16[3584,128]{1,0:T(8,128)(2,1)S(1)}, bf16[3584,128]{1,0:T(8,128)(2,1)S(1)}, u32[]{:S(2)}, u32[]{:S(2)}) collective-permute-start(bf16[3584,128]{1,0:T(8,128)(2,1)S(1)} %collective-permute-done.3), channel_id=1, source_target_pairs={{0,1},{1,0},{2,3},{3,2},{4,5},{5,4},{6,7},{7,6},{8,9},{9,8},{10,11... | collective-permute-start | bytes 2752520 | tf_op jit(solution)/shard_map/ppermute | solution.py:163
  85.0 34.3 %collective-permute-start.13 = (bf16[3456,128]{1,0:T(8,128)(2,1)S(1)}, bf16[3456,128]{1,0:T(8,128)(2,1)S(1)}, u32[]{:S(2)}, u32[]{:S(2)}) collective-permute-start(bf16[3456,128]{1,0:T(8,128)(2,1)S(1)} %collective-permute-done.5), channel_id=1, source_target_pairs={{0,1},{1,0},{2,3},{3,2},{4,5},{5,4},{6,7},{7,6},{8,9},{9,8},{10,11... | collective-permute-start | bytes 2654216 | tf_op jit(solution)/shard_map/ppermute | solution.py:163
  85.0 34.3 %collective-permute-start.14 = (bf16[3456,128]{1,0:T(8,128)(2,1)S(1)}, bf16[3456,128]{1,0:T(8,128)(2,1)S(1)}, u32[]{:S(2)}, u32[]{:S(2)}) collective-permute-start(bf16[3456,128]{1,0:T(8,128)(2,1)S(1)} %collective-permute-done.6), channel_id=1, source_target_pairs={{0,1},{1,0},{2,3},{3,2},{4,5},{5,4},{6,7},{7,6},{8,9},{9,8},{10,11... | collective-permute-start | bytes 2654216 | tf_op jit(solution)/shard_map/ppermute | solution.py:163
  85.5 33.8 %collective-permute-start.15 = (bf16[3072,128]{1,0:T(8,128)(2,1)S(1)}, bf16[3072,128]{1,0:T(8,128)(2,1)S(1)}, u32[]{:S(2)}, u32[]{:S(2)}) collective-permute-start(bf16[3072,128]{1,0:T(8,128)(2,1)S(1)} %collective-permute-done.7), channel_id=1, source_target_pairs={{0,1},{1,0},{2,3},{3,2},{4,5},{5,4},{6,7},{7,6},{8,9},{9,8},{10,11... | collective-permute-start | bytes 2359304 | tf_op jit(solution)/shard_map/ppermute | solution.py:163
  85.6 33.7 %collective-permute-start.16 = (bf16[3072,128]{1,0:T(8,128)(2,1)S(1)}, bf16[3072,128]{1,0:T(8,128)(2,1)S(1)}, u32[]{:S(2)}, u32[]{:S(2)}) collective-permute-start(bf16[3072,128]{1,0:T(8,128)(2,1)S(1)} %collective-permute-done.8), channel_id=1, source_target_pairs={{0,1},{1,0},{2,3},{3,2},{4,5},{5,4},{6,7},{7,6},{8,9},{9,8},{10,11... | collective-permute-start | bytes 2359304 | tf_op jit(solution)/shard_map/ppermute | solution.py:163
  (11 other events, 204.3 us)

commit v4 on v3

--- a/solution.py
+++ b/solution.py
@@ -13,10 +13,11 @@
 BLOCKS = 32
 SHARD = 8192
 RING = (2, -1, 1)
-LARGE, SMALLER = (1216, 672, 672), (832, 480, 480)
+LARGE, SMALLER = (1216, 640, 640), (832, 448, 448)
 BOTH = tuple(large + smaller for large, smaller in zip(LARGE, SMALLER))
 REST = SHARD - 4 * BOTH[1]
 ENTRIES = 8 * SHARD
+HELD = 8192
 SMALL = pltpu.CompilerParams(vmem_limit_bytes=8 << 20)
 
 
@@ -112,7 +113,7 @@
     return places
 
 
-def decode(me_ref, got_ref, *refs):
+def decode(me_ref, got_ref, held_ref, *refs):
     pieces, (out_ref, table_ref, pairs_ref, wide_ref, place_ref, scalar_ref, sem, place_sem) = refs[:-8], refs[-8:]
     me = me_ref[0]
     for piece, places in zip(pieces, table_parts(me, 0) + table_parts(me, 1)):
@@ -244,6 +245,10 @@
     return pl.BlockSpec(memory_space=pl.ANY)
 
 
+def hold(me_ref, held_ref):
+    held_ref[:16, :] = jnp.zeros((16, LANES), held_ref.dtype)
+
+
 def vmem():
     return pl.BlockSpec(memory_space=pltpu.VMEM)
 
@@ -276,6 +281,14 @@
         name="regroup",
     )(me, got)
     got = exchange(sent)
+    held = pl.pallas_call(
+        hold,
+        out_shape=pltpu.VMEM((HELD, LANES), jnp.bfloat16),
+        in_specs=[smem()],
+        out_specs=vmem(),
+        compiler_params=SMALL,
+        name="hold",
+    )(me)
     other_rest = [other_core(piece) for piece in rest]
     other_ring = [other_core(piece) for piece in ring[:2]]
     other_ring += [other_core(piece) for piece in ring[2:]]
@@ -284,7 +297,7 @@
     return pl.pallas_call(
         decode,
         out_shape=jax.ShapeDtypeStruct((BLOCKS * LANES, LANES), jnp.bfloat16),
-        in_specs=[smem(), vmem()] + [anywhere()] * len(pieces),
+        in_specs=[smem(), vmem(), vmem()] + [anywhere()] * len(pieces),
         out_specs=vmem(),
         scratch_shapes=[
             pltpu.VMEM((ENTRIES // 2 + 8, 2, LANES), jnp.bfloat16),
@@ -297,7 +310,7 @@
         ],
         compiler_params=pltpu.CompilerParams(vmem_limit_bytes=32 << 20),
         name="decode",
-    )(me, got, *pieces)
+    )(me, got, pltpu.with_memory_space_constraint(held, pltpu.VMEM), *pieces)
 
 
 def solution(mesh):

time: 136 us -> 138 us (1.015)
  blocking collectives: 31.3 us -> 17.7 us
  waiting for transfers between devices: 68.8 us -> 78.4 us
  starting transfers between devices: 15.4 us -> 21.4 us
    all_to_all x2 -> x1, blocking collectives: 31.3 us -> 17.7 us  [exchange(): return lax.all_to_all(x, ALL, 0, 0, tiled=True)]
    all_to_all x0 -> x1, waiting for transfers between devices: none -> 8.09 us  [exchange(): return lax.all_to_all(x, ALL, 0, 0, tiled=True)]
    all_to_all x0 -> x1, starting transfers between devices: none -> 5.97 us  [exchange(): return lax.all_to_all(x, ALL, 0, 0, tiled=True)]
    unnamed x36 -> x16, local copies, waits for them, and re-layouts: 2.24 us -> 0.53 us
    ppermute x17, waiting for transfers between devices: 68.8 us -> 70.3 us  [moved(): return lax.ppermute(x, ALL, pairs)]
  transfers between devices with their start and end apart: 17 -> 18, of which waited for: 3 -> 4; matrix products, arithmetic and copies ran while one was open for 0% -> 1% of each run, Pallas kernels for 2% -> 2%
where the time goes in v4:
time: 138 us; the launch traced here: 135 us
  waiting for transfers between devices  78.4 us (57%)
  starting transfers between devices  21.4 us (16%)
  blocking collectives  17.7 us (13%)
  Pallas kernels  16.1 us (12%)
  local copies, waits for them, and re-layouts  1.79 us (1%)
    ppermute x17, waiting for transfers between devices, moved(): return lax.ppermute(x, ALL, pairs)  70.3 us
    all_to_all x1, blocking collectives, exchange(): return lax.all_to_all(x, ALL, 0, 0, tiled=True)  17.7 us
    ppermute x17, starting transfers between devices, moved(): return lax.ppermute(x, ALL, pairs)  15.4 us
    pallas_call x1, Pallas kernels, steps(): pl.pallas_call(decode, out_shape=jax.ShapeDtypeStruct((BLOCKS * LANES, LA...  12 us
    all_to_all x1, waiting for transfers between devices, exchange(): return lax.all_to_all(x, ALL, 0, 0, tiled=True)  8.09 us
    all_to_all x1, starting transfers between devices, exchange(): return lax.all_to_all(x, ALL, 0, 0, tiled=True)  5.97 us
  transfers between devices with their start and end apart: 18, of which 4 were waited for; matrix products, arithmetic and copies ran while one was open for 1% of the time, Pallas kernels for 2%

profile of v4, /device:TPU:4, one launch (start us, length us, event | category | flops | bytes accessed | tf_op | source)
XLA Modules:
  0.0 135.5 jit_solution(3832416491171536670)
XLA Ops:
  0.0 1.2 cut.1
  1.2 4.0 %collective-permute-start = (bf16[2048,128]{1,0:T(8,128)(2,1)S(1)}, bf16[2048,128]{1,0:T(8,128)(2,1)S(1)}, u32[]{:S(2)}, u32[]{:S(2)}) collective-permute-start(bf16[2048,128]{1,0:T(8,128)(2,1)S(1)} %get-tuple-element.12), channel_id=1, source_target_pairs={{0,4},{1,5},{2,6},{3,7},{4,0},{5,1},{6,2},{7,3},{8,12},{9,13},{10,... | collective-permute-start | bytes 1572872 | tf_op jit(solution)/shard_map/ppermute | solution.py:164
  5.2 1.3 slice.3
  6.4 0.8 collective-permute-start.4
  7.2 1.3 collective-permute-start.3
  8.5 1.9 %collective-permute-start.2 = (bf16[1088,128]{1,0:T(8,128)(2,1)S(1)}, bf16[1088,128]{1,0:T(8,128)(2,1)S(1)}, u32[]{:S(2)}, u32[]{:S(2)}) collective-permute-start(bf16[1088,128]{1,0:T(8,128)(2,1)S(1)} %get-tuple-element.13), channel_id=1, source_target_pairs={{0,6},{1,7},{2,0},{3,1},{4,2},{5,3},{6,4},{7,5},{8,14},{9,15},{10,... | collective-permute-start | bytes 835592 | tf_op jit(solution)/shard_map/ppermute | solution.py:164
  10.6 34.3 %collective-permute-done.2.refs_2_ = bf16[1088,128]{1,0:T(8,128)(2,1)S(1)} collective-permute-done((bf16[1088,128]{1,0:T(8,128)(2,1)S(1)}, bf16[1088,128]{1,0:T(8,128)(2,1)S(1)}, u32[]{:S(2)}, u32[]{:S(2)}) %collective-permute-start.2) | collective-permute-done | bytes 278560 | tf_op jit(solution)/shard_map/ppermute | solution.py:164
  45.2 1.3 collective-permute-start.5
  46.5 1.6 %collective-permute-start.7 = (bf16[2976,128]{1,0:T(8,128)(2,1)S(1)}, bf16[2976,128]{1,0:T(8,128)(2,1)}, u32[]{:S(2)}, u32[]{:S(2)}) collective-permute-start(bf16[2976,128]{1,0:T(8,128)(2,1)S(1)} %get-tuple-element.17), channel_id=1, source_target_pairs={{0,32},{1,33},{2,34},{3,35},{4,36},{5,37},{6,38},{7,39},{8,40},{9,... | collective-permute-start | bytes 2285576 | tf_op jit(solution)/shard_map/ppermute | solution.py:164
  48.1 1.7 %collective-permute-start.8 = (bf16[2976,128]{1,0:T(8,128)(2,1)S(1)}, bf16[2976,128]{1,0:T(8,128)(2,1)}, u32[]{:S(2)}, u32[]{:S(2)}) collective-permute-start(bf16[2976,128]{1,0:T(8,128)(2,1)S(1)} %get-tuple-element.18), channel_id=1, source_target_pairs={{0,96},{1,97},{2,98},{3,99},{4,100},{5,101},{6,102},{7,103},{8,104... | collective-permute-start | bytes 2285576 | tf_op jit(solution)/shard_map/ppermute | solution.py:164
  49.8 0.5 collective-permute-start.10
  50.3 15.5 %collective-permute-done.7 = bf16[2976,128]{1,0:T(8,128)(2,1)} collective-permute-done((bf16[2976,128]{1,0:T(8,128)(2,1)S(1)}, bf16[2976,128]{1,0:T(8,128)(2,1)}, u32[]{:S(2)}, u32[]{:S(2)}) %collective-permute-start.7) | collective-permute-done | bytes 761888 | tf_op jit(solution)/shard_map/ppermute | solution.py:164
  65.8 0.5 collective-permute-start.11
  66.3 0.8 collective-permute-start.6
  67.1 20.4 %collective-permute-done.6 = bf16[3360,128]{1,0:T(8,128)(2,1)} collective-permute-done((bf16[3360,128]{1,0:T(8,128)(2,1)S(1)}, bf16[3360,128]{1,0:T(8,128)(2,1)}, u32[]{:S(2)}, u32[]{:S(2)}) %collective-permute-start.6) | collective-permute-done | bytes 860192 | tf_op jit(solution)/shard_map/ppermute | solution.py:164
  87.5 0.5 collective-permute-start.14
  88.1 0.4 collective-permute-start.16
  88.5 0.5 copy-done.6
  89.0 0.9 local_compaction.1
  90.0 17.7 %all_to_all.22 = s32[128,1,128]{2,1,0:T(1,128)S(1)} all-to-all(s32[128,1,128]{2,1,0:T(1,128)S(1)} %bitcast.30), channel_id=1, replica_groups=mesh['rows'=16,'dict'=8] {'rows','dict'}, dimensions={0} | all-to-all | bytes 131072 | tf_op jit(solution)/shard_map/all_to_all | solution.py:261
  107.6 1.7 %regroup.1 = s32[128,128]{1,0:T(8,128)} custom-call(s32[1]{0:T(128)} %bitcast.me_ref, s32[128,128]{1,0:T(8,128)S(1)} %bitcast.29), custom_call_target="tpu_custom_call" | custom-call | tf_op jit(solution)/shard_map/regroup/pallas_call | solution.py:275
  109.3 6.0 %all-to-all-start.1 = ((s32[128,1,128]{2,1,0:T(1,128)}), s32[128,1,128]{2,1,0:T(1,128)S(1)}, u32[]{:S(2)}, u32[]{:S(2)}) async-start(s32[128,1,128]{2,1,0:T(1,128)} %bitcast.7), calls=%async_computation.1 | async-start | bytes 131072 | tf_op jit(solution)/shard_map/all_to_all | solution.py:261
  115.3 8.1 %all-to-all-done.1 = s32[128,1,128]{2,1,0:T(1,128)S(1)} async-done(((s32[128,1,128]{2,1,0:T(1,128)}), s32[128,1,128]{2,1,0:T(1,128)S(1)}, u32[]{:S(2)}, u32[]{:S(2)}) %all-to-all-start.1) | async-done | bytes 65568 | tf_op jit(solution)/shard_map/all_to_all | solution.py:261
  123.4 12.0 %decode.1 = bf16[4096,128]{1,0:T(8,128)(2,1)} custom-call(s32[1]{0:T(128)} %bitcast.me_ref, s32[128,128]{1,0:T(8,128)S(1)} %bitcast.28, bf16[8192,128]{1,0:T(8,128)(2,1)S(1)} %hold.1.held_ref, bf16[4096,2,128]{2,1,0:T(2,128)(2,1)} %bitcast.9.refs_0_, bf16[2112,2,128]{2,1,0:T(2,128)(2,1)} %bitcast.27, bf16[1920,2,128]{2,1,0:T(2,128)(2,1)} %bitcast.35, ...), custom_call_target="tpu_custom_call" | custom-call | tf_op jit(solution)/shard_map/decode/pallas_call | solution.py:297
  (36 shorter events, 0.6 us)
Async XLA Ops:
  0.0 89.0 %copy-start.1 = (s32[4096]{0:T(1024)S(1)}, s32[4096]{0:T(1024)}, u32[]{:S(2)}) copy-start(s32[4096]{0:T(1024)} %param.3) | copy-start | bytes 49156
  0.0 89.0 %copy-start.2 = (s32[4096]{0:T(1024)S(1)}, s32[4096]{0:T(1024)}, u32[]{:S(2)}) copy-start(s32[4096]{0:T(1024)} %param.4) | copy-start | bytes 49156
  1.2 43.7 %collective-permute-start = (bf16[2048,128]{1,0:T(8,128)(2,1)S(1)}, bf16[2048,128]{1,0:T(8,128)(2,1)S(1)}, u32[]{:S(2)}, u32[]{:S(2)}) collective-permute-start(bf16[2048,128]{1,0:T(8,128)(2,1)S(1)} %get-tuple-element.12), channel_id=1, source_target_pairs={{0,4},{1,5},{2,6},{3,7},{4,0},{5,1},{6,2},{7,3},{8,12},{9,13},{10,... | collective-permute-start | bytes 1572872 | tf_op jit(solution)/shard_map/ppermute | solution.py:164
  6.4 43.3 %collective-permute-start.4 = (bf16[3840,128]{1,0:T(8,128)(2,1)S(1)}, bf16[3840,128]{1,0:T(8,128)(2,1)S(1)}, u32[]{:S(2)}, u32[]{:S(2)}) collective-permute-start(bf16[3840,128]{1,0:T(8,128)(2,1)S(1)} %slice.3), channel_id=1, source_target_pairs={{0,6},{1,7},{2,0},{3,1},{4,2},{5,3},{6,4},{7,5},{8,14},{9,15},{10,... | collective-permute-start | bytes 2949128 | tf_op jit(solution)/shard_map/ppermute | solution.py:164
  7.2 42.6 %collective-permute-start.3 = (bf16[3840,128]{1,0:T(8,128)(2,1)S(1)}, bf16[3840,128]{1,0:T(8,128)(2,1)S(1)}, u32[]{:S(2)}, u32[]{:S(2)}) collective-permute-start(bf16[3840,128]{1,0:T(8,128)(2,1)S(1)} %slice.3), channel_id=1, source_target_pairs={{0,2},{1,3},{2,4},{3,5},{4,6},{5,7},{6,0},{7,1},{8,10},{9,11},{10,... | collective-permute-start | bytes 2949128 | tf_op jit(solution)/shard_map/ppermute | solution.py:164
  8.5 36.4 %collective-permute-start.2 = (bf16[1088,128]{1,0:T(8,128)(2,1)S(1)}, bf16[1088,128]{1,0:T(8,128)(2,1)S(1)}, u32[]{:S(2)}, u32[]{:S(2)}) collective-permute-start(bf16[1088,128]{1,0:T(8,128)(2,1)S(1)} %get-tuple-element.13), channel_id=1, source_target_pairs={{0,6},{1,7},{2,0},{3,1},{4,2},{5,3},{6,4},{7,5},{8,14},{9,15},{10,... | collective-permute-start | bytes 835592 | tf_op jit(solution)/shard_map/ppermute | solution.py:164
  10.4 34.4 %collective-permute-start.1 = (bf16[1088,128]{1,0:T(8,128)(2,1)S(1)}, bf16[1088,128]{1,0:T(8,128)(2,1)S(1)}, u32[]{:S(2)}, u32[]{:S(2)}) collective-permute-start(bf16[1088,128]{1,0:T(8,128)(2,1)S(1)} %get-tuple-element.13), channel_id=1, source_target_pairs={{0,2},{1,3},{2,4},{3,5},{4,6},{5,7},{6,0},{7,1},{8,10},{9,11},{10,... | collective-permute-start | bytes 835592 | tf_op jit(solution)/shard_map/ppermute | solution.py:164
  45.2 78.2 %copy-start = (bf16[4224,128]{1,0:T(8,128)(2,1)}, bf16[4224,128]{1,0:T(8,128)(2,1)S(1)}, u32[]{:S(2)}) copy-start(bf16[4224,128]{1,0:T(8,128)(2,1)S(1)} %get-tuple-element.14) | copy-start | bytes 3244036
  45.2 21.0 %collective-permute-start.5 = (bf16[3360,128]{1,0:T(8,128)(2,1)S(1)}, bf16[3360,128]{1,0:T(8,128)(2,1)}, u32[]{:S(2)}, u32[]{:S(2)}) collective-permute-start(bf16[3360,128]{1,0:T(8,128)(2,1)S(1)} %get-tuple-element.15), channel_id=1, source_target_pairs={{0,8},{1,9},{2,10},{3,11},{4,12},{5,13},{6,14},{7,15},{8,16},{9,17... | collective-permute-start | bytes 2580488 | tf_op jit(solution)/shard_map/ppermute | solution.py:164
  46.5 19.3 %collective-permute-start.7 = (bf16[2976,128]{1,0:T(8,128)(2,1)S(1)}, bf16[2976,128]{1,0:T(8,128)(2,1)}, u32[]{:S(2)}, u32[]{:S(2)}) collective-permute-start(bf16[2976,128]{1,0:T(8,128)(2,1)S(1)} %get-tuple-element.17), channel_id=1, source_target_pairs={{0,32},{1,33},{2,34},{3,35},{4,36},{5,37},{6,38},{7,39},{8,40},{9,... | collective-permute-start | bytes 2285576 | tf_op jit(solution)/shard_map/ppermute | solution.py:164
  48.1 17.7 %collective-permute-start.8 = (bf16[2976,128]{1,0:T(8,128)(2,1)S(1)}, bf16[2976,128]{1,0:T(8,128)(2,1)}, u32[]{:S(2)}, u32[]{:S(2)}) collective-permute-start(bf16[2976,128]{1,0:T(8,128)(2,1)S(1)} %get-tuple-element.18), channel_id=1, source_target_pairs={{0,96},{1,97},{2,98},{3,99},{4,100},{5,101},{6,102},{7,103},{8,104... | collective-permute-start | bytes 2285576 | tf_op jit(solution)/shard_map/ppermute | solution.py:164
  49.8 59.5 %copy-start.4 = (bf16[3840,128]{1,0:T(8,128)(2,1)}, bf16[3840,128]{1,0:T(8,128)(2,1)S(1)}, u32[]{:S(2)}) copy-start(bf16[3840,128]{1,0:T(8,128)(2,1)S(1)} %collective-permute-done.4) | copy-start | bytes 2949124
  49.8 73.6 %collective-permute-start.9 = (bf16[8192,128]{1,0:T(8,128)(2,1)}, bf16[8192,128]{1,0:T(8,128)(2,1)}, u32[]{:S(2)}, u32[]{:S(2)}) collective-permute-start(bf16[8192,128]{1,0:T(8,128)(2,1)} %table_ref.1), channel_id=1, source_target_pairs={{0,1},{1,0},{2,3},{3,2},{4,5},{5,4},{6,7},{7,6},{8,9},{9,8},{10,11... | collective-permute-start | bytes 6291464 | tf_op jit(solution)/shard_map/ppermute | solution.py:164
  49.8 59.5 %copy-start.5 = (bf16[3840,128]{1,0:T(8,128)(2,1)}, bf16[3840,128]{1,0:T(8,128)(2,1)S(1)}, u32[]{:S(2)}) copy-start(bf16[3840,128]{1,0:T(8,128)(2,1)S(1)} %collective-permute-done.3) | copy-start | bytes 2949124
  49.8 37.7 %collective-permute-start.10 = (bf16[4224,128]{1,0:T(8,128)(2,1)S(1)}, bf16[4224,128]{1,0:T(8,128)(2,1)S(1)}, u32[]{:S(2)}, u32[]{:S(2)}) collective-permute-start(bf16[4224,128]{1,0:T(8,128)(2,1)S(1)} %get-tuple-element.14), channel_id=1, source_target_pairs={{0,1},{1,0},{2,3},{3,2},{4,5},{5,4},{6,7},{7,6},{8,9},{9,8},{10,11... | collective-permute-start | bytes 3244040 | tf_op jit(solution)/shard_map/ppermute | solution.py:164
  65.8 22.2 %collective-permute-start.12 = (bf16[3840,128]{1,0:T(8,128)(2,1)S(1)}, bf16[3840,128]{1,0:T(8,128)(2,1)S(1)}, u32[]{:S(2)}, u32[]{:S(2)}) collective-permute-start(bf16[3840,128]{1,0:T(8,128)(2,1)S(1)} %collective-permute-done.4), channel_id=1, source_target_pairs={{0,1},{1,0},{2,3},{3,2},{4,5},{5,4},{6,7},{7,6},{8,9},{9,8},{10,11... | collective-permute-start | bytes 2949128 | tf_op jit(solution)/shard_map/ppermute | solution.py:164
  65.8 22.3 %collective-permute-start.11 = (bf16[3840,128]{1,0:T(8,128)(2,1)S(1)}, bf16[3840,128]{1,0:T(8,128)(2,1)S(1)}, u32[]{:S(2)}, u32[]{:S(2)}) collective-permute-start(bf16[3840,128]{1,0:T(8,128)(2,1)S(1)} %collective-permute-done.3), channel_id=1, source_target_pairs={{0,1},{1,0},{2,3},{3,2},{4,5},{5,4},{6,7},{7,6},{8,9},{9,8},{10,11... | collective-permute-start | bytes 2949128 | tf_op jit(solution)/shard_map/ppermute | solution.py:164
  66.3 21.2 %collective-permute-start.6 = (bf16[3360,128]{1,0:T(8,128)(2,1)S(1)}, bf16[3360,128]{1,0:T(8,128)(2,1)}, u32[]{:S(2)}, u32[]{:S(2)}) collective-permute-start(bf16[3360,128]{1,0:T(8,128)(2,1)S(1)} %get-tuple-element.16), channel_id=1, source_target_pairs={{0,24},{1,25},{2,26},{3,27},{4,28},{5,29},{6,30},{7,31},{8,0},{9,1... | collective-permute-start | bytes 2580488 | tf_op jit(solution)/shard_map/ppermute | solution.py:164
  87.5 35.9 %collective-permute-start.13 = (bf16[3360,128]{1,0:T(8,128)(2,1)}, bf16[3360,128]{1,0:T(8,128)(2,1)}, u32[]{:S(2)}, u32[]{:S(2)}) collective-permute-start(bf16[3360,128]{1,0:T(8,128)(2,1)} %collective-permute-done.5), channel_id=1, source_target_pairs={{0,1},{1,0},{2,3},{3,2},{4,5},{5,4},{6,7},{7,6},{8,9},{9,8},{10,11... | collective-permute-start | bytes 2580488 | tf_op jit(solution)/shard_map/ppermute | solution.py:164
  87.5 35.9 %collective-permute-start.14 = (bf16[3360,128]{1,0:T(8,128)(2,1)}, bf16[3360,128]{1,0:T(8,128)(2,1)}, u32[]{:S(2)}, u32[]{:S(2)}) collective-permute-start(bf16[3360,128]{1,0:T(8,128)(2,1)} %collective-permute-done.6), channel_id=1, source_target_pairs={{0,1},{1,0},{2,3},{3,2},{4,5},{5,4},{6,7},{7,6},{8,9},{9,8},{10,11... | collective-permute-start | bytes 2580488 | tf_op jit(solution)/shard_map/ppermute | solution.py:164
  88.0 35.4 %collective-permute-start.15 = (bf16[2976,128]{1,0:T(8,128)(2,1)}, bf16[2976,128]{1,0:T(8,128)(2,1)}, u32[]{:S(2)}, u32[]{:S(2)}) collective-permute-start(bf16[2976,128]{1,0:T(8,128)(2,1)} %collective-permute-done.7), channel_id=1, source_target_pairs={{0,1},{1,0},{2,3},{3,2},{4,5},{5,4},{6,7},{7,6},{8,9},{9,8},{10,11... | collective-permute-start | bytes 2285576 | tf_op jit(solution)/shard_map/ppermute | solution.py:164
  88.1 21.2 %copy-start.7 = (bf16[3840,128]{1,0:T(8,128)(2,1)}, bf16[3840,128]{1,0:T(8,128)(2,1)S(1)}, u32[]{:S(2)}) copy-start(bf16[3840,128]{1,0:T(8,128)(2,1)S(1)} %collective-permute-done.11) | copy-start | bytes 2949124
  88.1 35.3 %collective-permute-start.16 = (bf16[2976,128]{1,0:T(8,128)(2,1)}, bf16[2976,128]{1,0:T(8,128)(2,1)}, u32[]{:S(2)}, u32[]{:S(2)}) collective-permute-start(bf16[2976,128]{1,0:T(8,128)(2,1)} %collective-permute-done.8), channel_id=1, source_target_pairs={{0,1},{1,0},{2,3},{3,2},{4,5},{5,4},{6,7},{7,6},{8,9},{9,8},{10,11... | collective-permute-start | bytes 2285576 | tf_op jit(solution)/shard_map/ppermute | solution.py:164
  109.3 14.1 %all-to-all-start.1 = ((s32[128,1,128]{2,1,0:T(1,128)}), s32[128,1,128]{2,1,0:T(1,128)S(1)}, u32[]{:S(2)}, u32[]{:S(2)}) async-start(s32[128,1,128]{2,1,0:T(1,128)} %bitcast.7), calls=%async_computation.1 | async-start | bytes 131072 | tf_op jit(solution)/shard_map/all_to_all | solution.py:261
  (2 other events, 2.1 us)

commit v5 on v4

--- a/solution.py
+++ b/solution.py
@@ -13,7 +13,7 @@
 BLOCKS = 32
 SHARD = 8192
 RING = (2, -1, 1)
-LARGE, SMALLER = (1216, 640, 640), (832, 448, 448)
+LARGE, SMALLER = (1248, 608, 608), (800, 416, 416)
 BOTH = tuple(large + smaller for large, smaller in zip(LARGE, SMALLER))
 REST = SHARD - 4 * BOTH[1]
 ENTRIES = 8 * SHARD
@@ -114,7 +114,8 @@
 
 
 def decode(me_ref, got_ref, held_ref, *refs):
-    pieces, (out_ref, table_ref, pairs_ref, wide_ref, place_ref, scalar_ref, sem, place_sem) = refs[:-8], refs[-8:]
+    pieces, out_ref, scratch = refs[:-11], refs[-11], refs[-10:]
+    table_ref, pairs_ref, wide_ref, odd_ref, rows_ref, place_ref, scalar_ref, sem, place_sem, out_sem = scratch
     me = me_ref[0]
     for piece, places in zip(pieces, table_parts(me, 0) + table_parts(me, 1)):
         at = 0
@@ -137,22 +138,35 @@
     to_scalars = pltpu.make_async_copy(place_ref, scalar_ref, place_sem)
     to_scalars.start()
     odd = jnp.concatenate([item & 1, jnp.zeros((LANES - BLOCKS, LANES), jnp.int32)], axis=0).T
+    for b in range(BLOCKS):
+        odd_ref[b] = jnp.broadcast_to(odd[:, b : b + 1], (LANES, LANES))
+    pairs_ref[0] = jnp.zeros(pairs_ref.shape[1:], pairs_ref.dtype)
     to_scalars.wait()
     filled = table_ref.at[pl.ds(0, ENTRIES // 2)]
     pltpu.make_async_copy(filled, filled, sem).wait()
 
+    def finish(b):
+        wide_ref[...] = pairs_ref[b].astype(jnp.float32)
+        second, first = wide_ref[pl.ds(1, LANES, stride=2), :], wide_ref[pl.ds(0, LANES, stride=2), :]
+        row = jnp.where(odd_ref[b] == 1, second, first)
+        rows_ref[b] = row.astype(rows_ref.dtype)
+
+    def send(b):
+        here = out_ref.at[pl.ds(pl.multiple_of(b * LANES, LANES), LANES)]
+        pltpu.make_async_copy(rows_ref.at[b], here, out_sem).start()
+
     def fetch(b, _):
+        before = jnp.maximum(b - 1, 0)
+        finish(before)
         for j in range(LANES):
             pairs_ref[b, 2 * j : 2 * j + 2, :] = table_ref[scalar_ref[b, j]]
+        pl.when(b > 0)(lambda: send(before))
         return 0
 
     lax.fori_loop(0, BLOCKS, fetch, 0)
-    for b in range(BLOCKS):
-        wide = wide_ref.at[b % 4]
-        wide[...] = pairs_ref[b].astype(jnp.float32)
-        second = jnp.broadcast_to(odd[:, b : b + 1], (LANES, LANES)) == 1
-        row = jnp.where(second, wide[pl.ds(1, LANES, stride=2), :], wide[pl.ds(0, LANES, stride=2), :])
-        out_ref[b * LANES : (b + 1) * LANES, :] = row.astype(out_ref.dtype)
+    finish(BLOCKS - 1)
+    send(BLOCKS - 1)
+    pltpu.make_async_copy(out_ref, out_ref, out_sem).wait()
 
 
 def moved(x, by):
@@ -289,7 +303,9 @@
         compiler_params=SMALL,
         name="hold",
     )(me)
-    other_rest = [other_core(piece) for piece in rest]
+    other_rest = []
+    for piece in rest:
+        other_rest.append(other_core(piece))
     other_ring = [other_core(piece) for piece in ring[:2]]
     other_ring += [other_core(piece) for piece in ring[2:]]
     pieces = [decoding_table, every, *rest, *ring, other_table, other_every, *other_rest, *other_ring]
@@ -298,13 +314,16 @@
         decode,
         out_shape=jax.ShapeDtypeStruct((BLOCKS * LANES, LANES), jnp.bfloat16),
         in_specs=[smem(), vmem(), vmem()] + [anywhere()] * len(pieces),
-        out_specs=vmem(),
+        out_specs=anywhere(),
         scratch_shapes=[
             pltpu.VMEM((ENTRIES // 2 + 8, 2, LANES), jnp.bfloat16),
             pltpu.VMEM((BLOCKS, 2 * LANES, LANES), jnp.bfloat16),
-            pltpu.VMEM((4, 2 * LANES, LANES), jnp.float32),
+            pltpu.VMEM((2 * LANES, LANES), jnp.float32),
+            pltpu.VMEM((BLOCKS, LANES, LANES), jnp.int32),
+            pltpu.VMEM((BLOCKS, LANES, LANES), jnp.bfloat16),
             pltpu.VMEM((BLOCKS, LANES), jnp.int32),
             pltpu.SMEM((BLOCKS, LANES), jnp.int32),
+            pltpu.SemaphoreType.DMA(()),
             pltpu.SemaphoreType.DMA(()),
             pltpu.SemaphoreType.DMA(()),
         ],

time: 138 us -> 134 us (0.971)
  waiting for transfers between devices: 78.4 us -> 75.9 us
    ppermute x17, waiting for transfers between devices: 70.3 us -> 67.9 us  [moved(): return lax.ppermute(x, ALL, pairs)]
  transfers between devices with their start and end apart: 18 -> 18, of which waited for: 4 -> 6; matrix products, arithmetic and copies ran while one was open for 1% -> 1% of each run, Pallas kernels for 2% -> 2%
where the time goes in v5:
time: 134 us; the launch traced here: 132 us
  waiting for transfers between devices  75.9 us (57%)
  starting transfers between devices  20.6 us (15%)
  blocking collectives  18.2 us (14%)
  Pallas kernels  15.5 us (12%)
    ppermute x17, waiting for transfers between devices, moved(): return lax.ppermute(x, ALL, pairs)  67.9 us
    all_to_all x1, blocking collectives, exchange(): return lax.all_to_all(x, ALL, 0, 0, tiled=True)  18.2 us
    ppermute x17, starting transfers between devices, moved(): return lax.ppermute(x, ALL, pairs)  14.6 us
    pallas_call x1, Pallas kernels, steps(): pl.pallas_call(decode, out_shape=jax.ShapeDtypeStruct((BLOCKS * LANES, LA...  11.4 us
    all_to_all x1, waiting for transfers between devices, exchange(): return lax.all_to_all(x, ALL, 0, 0, tiled=True)  8.09 us
    all_to_all x1, starting transfers between devices, exchange(): return lax.all_to_all(x, ALL, 0, 0, tiled=True)  5.97 us
  transfers between devices with their start and end apart: 18, of which 6 were waited for; matrix products, arithmetic and copies ran while one was open for 1% of the time, Pallas kernels for 2%

profile of v5, /device:TPU:4, one launch (start us, length us, event | category | flops | bytes accessed | tf_op | source)
XLA Modules:
  0.0 131.8 jit_solution(9772482532562533962)
XLA Ops:
  0.0 1.2 cut.1
  1.2 4.0 %collective-permute-start = (bf16[2048,128]{1,0:T(8,128)(2,1)S(1)}, bf16[2048,128]{1,0:T(8,128)(2,1)S(1)}, u32[]{:S(2)}, u32[]{:S(2)}) collective-permute-start(bf16[2048,128]{1,0:T(8,128)(2,1)S(1)} %get-tuple-element.12), channel_id=1, source_target_pairs={{0,4},{1,5},{2,6},{3,7},{4,0},{5,1},{6,2},{7,3},{8,12},{9,13},{10,... | collective-permute-start | bytes 1572872 | tf_op jit(solution)/shard_map/ppermute | solution.py:178
  5.2 1.3 slice.3
  6.5 0.8 collective-permute-start.4
  7.2 1.3 collective-permute-start.3
  8.6 1.9 %collective-permute-start.2 = (bf16[1024,128]{1,0:T(8,128)(2,1)S(1)}, bf16[1024,128]{1,0:T(8,128)(2,1)S(1)}, u32[]{:S(2)}, u32[]{:S(2)}) collective-permute-start(bf16[1024,128]{1,0:T(8,128)(2,1)S(1)} %get-tuple-element.13), channel_id=1, source_target_pairs={{0,6},{1,7},{2,0},{3,1},{4,2},{5,3},{6,4},{7,5},{8,14},{9,15},{10,... | collective-permute-start | bytes 786440 | tf_op jit(solution)/shard_map/ppermute | solution.py:178
  10.6 35.4 %collective-permute-done.2.refs_2_ = bf16[1024,128]{1,0:T(8,128)(2,1)S(1)} collective-permute-done((bf16[1024,128]{1,0:T(8,128)(2,1)S(1)}, bf16[1024,128]{1,0:T(8,128)(2,1)S(1)}, u32[]{:S(2)}, u32[]{:S(2)}) %collective-permute-start.2) | collective-permute-done | bytes 262176 | tf_op jit(solution)/shard_map/ppermute | solution.py:178
  46.3 1.6 %collective-permute-start.7 = (bf16[2864,128]{1,0:T(8,128)(2,1)S(1)}, bf16[2864,128]{1,0:T(8,128)(2,1)S(1)}, u32[]{:S(2)}, u32[]{:S(2)}) collective-permute-start(bf16[2864,128]{1,0:T(8,128)(2,1)S(1)} %get-tuple-element.17), channel_id=1, source_target_pairs={{0,32},{1,33},{2,34},{3,35},{4,36},{5,37},{6,38},{7,39},{8,40},{9,... | collective-permute-start | bytes 2199560 | tf_op jit(solution)/shard_map/ppermute | solution.py:178
  47.9 1.2 collective-permute-start.5
  49.1 1.7 %collective-permute-start.8 = (bf16[2864,128]{1,0:T(8,128)(2,1)S(1)}, bf16[2864,128]{1,0:T(8,128)(2,1)S(1)}, u32[]{:S(2)}, u32[]{:S(2)}) collective-permute-start(bf16[2864,128]{1,0:T(8,128)(2,1)S(1)} %get-tuple-element.18), channel_id=1, source_target_pairs={{0,96},{1,97},{2,98},{3,99},{4,100},{5,101},{6,102},{7,103},{8,104... | collective-permute-start | bytes 2199560 | tf_op jit(solution)/shard_map/ppermute | solution.py:178
  50.8 0.5 collective-permute-start.9
  51.3 13.9 %collective-permute-done.7 = bf16[2864,128]{1,0:T(8,128)(2,1)S(1)} collective-permute-done((bf16[2864,128]{1,0:T(8,128)(2,1)S(1)}, bf16[2864,128]{1,0:T(8,128)(2,1)S(1)}, u32[]{:S(2)}, u32[]{:S(2)}) %collective-permute-start.7) | collective-permute-done | bytes 733216 | tf_op jit(solution)/shard_map/ppermute | solution.py:178
  65.2 0.5 collective-permute-start.6
  65.7 0.4 collective-permute-done.8
  66.1 1.5 %collective-permute-done.5 = bf16[3280,128]{1,0:T(8,128)(2,1)} collective-permute-done((bf16[3280,128]{1,0:T(8,128)(2,1)S(1)}, bf16[3280,128]{1,0:T(8,128)(2,1)}, u32[]{:S(2)}, u32[]{:S(2)}) %collective-permute-start.5) | collective-permute-done | bytes 839712 | tf_op jit(solution)/shard_map/ppermute | solution.py:178
  67.6 16.7 %collective-permute-done.6 = bf16[3280,128]{1,0:T(8,128)(2,1)} collective-permute-done((bf16[3280,128]{1,0:T(8,128)(2,1)S(1)}, bf16[3280,128]{1,0:T(8,128)(2,1)}, u32[]{:S(2)}, u32[]{:S(2)}) %collective-permute-start.6) | collective-permute-done | bytes 839712 | tf_op jit(solution)/shard_map/ppermute | solution.py:178
  84.3 0.5 collective-permute-start.11
  84.9 0.4 collective-permute-start.14
  85.4 0.9 local_compaction.1
  86.3 18.2 %all_to_all.22 = s32[128,1,128]{2,1,0:T(1,128)S(1)} all-to-all(s32[128,1,128]{2,1,0:T(1,128)S(1)} %bitcast.30), channel_id=1, replica_groups=mesh['rows'=16,'dict'=8] {'rows','dict'}, dimensions={0} | all-to-all | bytes 131072 | tf_op jit(solution)/shard_map/all_to_all | solution.py:275
  104.5 1.7 %regroup.1 = s32[128,128]{1,0:T(8,128)} custom-call(s32[1]{0:T(128)} %bitcast.me_ref, s32[128,128]{1,0:T(8,128)S(1)} %bitcast.29), custom_call_target="tpu_custom_call" | custom-call | tf_op jit(solution)/shard_map/regroup/pallas_call | solution.py:289
  106.2 6.0 %all-to-all-start.1 = ((s32[128,1,128]{2,1,0:T(1,128)}), s32[128,1,128]{2,1,0:T(1,128)S(1)}, u32[]{:S(2)}, u32[]{:S(2)}) async-start(s32[128,1,128]{2,1,0:T(1,128)} %bitcast.7), calls=%async_computation.1 | async-start | bytes 131072 | tf_op jit(solution)/shard_map/all_to_all | solution.py:275
  112.2 8.1 %all-to-all-done.1 = s32[128,1,128]{2,1,0:T(1,128)S(1)} async-done(((s32[128,1,128]{2,1,0:T(1,128)}), s32[128,1,128]{2,1,0:T(1,128)S(1)}, u32[]{:S(2)}, u32[]{:S(2)}) %all-to-all-start.1) | async-done | bytes 65568 | tf_op jit(solution)/shard_map/all_to_all | solution.py:275
  120.3 11.4 %decode.1 = bf16[4096,128]{1,0:T(8,128)(2,1)} custom-call(s32[1]{0:T(128)} %bitcast.me_ref, s32[128,128]{1,0:T(8,128)S(1)} %bitcast.28, bf16[8192,128]{1,0:T(8,128)(2,1)S(1)} %hold.1.held_ref, bf16[4096,2,128]{2,1,0:T(2,128)(2,1)} %bitcast.9.refs_0_, bf16[2048,2,128]{2,1,0:T(2,128)(2,1)} %bitcast.27, bf16[2048,2,128]{2,1,0:T(2,128)(2,1)} %bitcast.11.refs_2_, ...), custom_call_target="tpu_custom_call" | custom-call | tf_op jit(solution)/shard_map/decode/pallas_call | solution.py:313
  (36 shorter events, 0.6 us)
Async XLA Ops:
  1.2 84.2 %copy-start.1 = (s32[4096]{0:T(1024)S(1)}, s32[4096]{0:T(1024)}, u32[]{:S(2)}) copy-start(s32[4096]{0:T(1024)} %param.3) | copy-start | bytes 49156
  1.2 84.2 %copy-start.2 = (s32[4096]{0:T(1024)S(1)}, s32[4096]{0:T(1024)}, u32[]{:S(2)}) copy-start(s32[4096]{0:T(1024)} %param.4) | copy-start | bytes 49156
  1.2 44.8 %collective-permute-start = (bf16[2048,128]{1,0:T(8,128)(2,1)S(1)}, bf16[2048,128]{1,0:T(8,128)(2,1)S(1)}, u32[]{:S(2)}, u32[]{:S(2)}) collective-permute-start(bf16[2048,128]{1,0:T(8,128)(2,1)S(1)} %get-tuple-element.12), channel_id=1, source_target_pairs={{0,4},{1,5},{2,6},{3,7},{4,0},{5,1},{6,2},{7,3},{8,12},{9,13},{10,... | collective-permute-start | bytes 1572872 | tf_op jit(solution)/shard_map/ppermute | solution.py:178
  6.5 44.3 %collective-permute-start.4 = (bf16[4096,128]{1,0:T(8,128)(2,1)S(1)}, bf16[4096,128]{1,0:T(8,128)(2,1)}, u32[]{:S(2)}, u32[]{:S(2)}) collective-permute-start(bf16[4096,128]{1,0:T(8,128)(2,1)S(1)} %slice.3), channel_id=1, source_target_pairs={{0,6},{1,7},{2,0},{3,1},{4,2},{5,3},{6,4},{7,5},{8,14},{9,15},{10,... | collective-permute-start | bytes 3145736 | tf_op jit(solution)/shard_map/ppermute | solution.py:178
  7.2 43.6 %collective-permute-start.3 = (bf16[4096,128]{1,0:T(8,128)(2,1)S(1)}, bf16[4096,128]{1,0:T(8,128)(2,1)}, u32[]{:S(2)}, u32[]{:S(2)}) collective-permute-start(bf16[4096,128]{1,0:T(8,128)(2,1)S(1)} %slice.3), channel_id=1, source_target_pairs={{0,2},{1,3},{2,4},{3,5},{4,6},{5,7},{6,0},{7,1},{8,10},{9,11},{10,... | collective-permute-start | bytes 3145736 | tf_op jit(solution)/shard_map/ppermute | solution.py:178
  8.6 37.4 %collective-permute-start.2 = (bf16[1024,128]{1,0:T(8,128)(2,1)S(1)}, bf16[1024,128]{1,0:T(8,128)(2,1)S(1)}, u32[]{:S(2)}, u32[]{:S(2)}) collective-permute-start(bf16[1024,128]{1,0:T(8,128)(2,1)S(1)} %get-tuple-element.13), channel_id=1, source_target_pairs={{0,6},{1,7},{2,0},{3,1},{4,2},{5,3},{6,4},{7,5},{8,14},{9,15},{10,... | collective-permute-start | bytes 786440 | tf_op jit(solution)/shard_map/ppermute | solution.py:178
  10.5 35.5 %collective-permute-start.1 = (bf16[1024,128]{1,0:T(8,128)(2,1)S(1)}, bf16[1024,128]{1,0:T(8,128)(2,1)S(1)}, u32[]{:S(2)}, u32[]{:S(2)}) collective-permute-start(bf16[1024,128]{1,0:T(8,128)(2,1)S(1)} %get-tuple-element.13), channel_id=1, source_target_pairs={{0,2},{1,3},{2,4},{3,5},{4,6},{5,7},{6,0},{7,1},{8,10},{9,11},{10,... | collective-permute-start | bytes 786440 | tf_op jit(solution)/shard_map/ppermute | solution.py:178
  46.3 74.1 %copy-start = (bf16[4096,128]{1,0:T(8,128)(2,1)}, bf16[4096,128]{1,0:T(8,128)(2,1)S(1)}, u32[]{:S(2)}) copy-start(bf16[4096,128]{1,0:T(8,128)(2,1)S(1)} %get-tuple-element.14) | copy-start | bytes 3145732
  46.3 18.9 %collective-permute-start.7 = (bf16[2864,128]{1,0:T(8,128)(2,1)S(1)}, bf16[2864,128]{1,0:T(8,128)(2,1)S(1)}, u32[]{:S(2)}, u32[]{:S(2)}) collective-permute-start(bf16[2864,128]{1,0:T(8,128)(2,1)S(1)} %get-tuple-element.17), channel_id=1, source_target_pairs={{0,32},{1,33},{2,34},{3,35},{4,36},{5,37},{6,38},{7,39},{8,40},{9,... | collective-permute-start | bytes 2199560 | tf_op jit(solution)/shard_map/ppermute | solution.py:178
  47.9 19.6 %collective-permute-start.5 = (bf16[3280,128]{1,0:T(8,128)(2,1)S(1)}, bf16[3280,128]{1,0:T(8,128)(2,1)}, u32[]{:S(2)}, u32[]{:S(2)}) collective-permute-start(bf16[3280,128]{1,0:T(8,128)(2,1)S(1)} %get-tuple-element.15), channel_id=1, source_target_pairs={{0,8},{1,9},{2,10},{3,11},{4,12},{5,13},{6,14},{7,15},{8,16},{9,17... | collective-permute-start | bytes 2519048 | tf_op jit(solution)/shard_map/ppermute | solution.py:178
  49.1 17.0 %collective-permute-start.8 = (bf16[2864,128]{1,0:T(8,128)(2,1)S(1)}, bf16[2864,128]{1,0:T(8,128)(2,1)S(1)}, u32[]{:S(2)}, u32[]{:S(2)}) collective-permute-start(bf16[2864,128]{1,0:T(8,128)(2,1)S(1)} %get-tuple-element.18), channel_id=1, source_target_pairs={{0,96},{1,97},{2,98},{3,99},{4,100},{5,101},{6,102},{7,103},{8,104... | collective-permute-start | bytes 2199560 | tf_op jit(solution)/shard_map/ppermute | solution.py:178
  50.8 33.5 %collective-permute-start.10 = (bf16[4096,128]{1,0:T(8,128)(2,1)S(1)}, bf16[4096,128]{1,0:T(8,128)(2,1)S(1)}, u32[]{:S(2)}, u32[]{:S(2)}) collective-permute-start(bf16[4096,128]{1,0:T(8,128)(2,1)S(1)} %get-tuple-element.14), channel_id=1, source_target_pairs={{0,1},{1,0},{2,3},{3,2},{4,5},{5,4},{6,7},{7,6},{8,9},{9,8},{10,11... | collective-permute-start | bytes 3145736 | tf_op jit(solution)/shard_map/ppermute | solution.py:178
  50.8 69.5 %collective-permute-start.9 = (bf16[8192,128]{1,0:T(8,128)(2,1)}, bf16[8192,128]{1,0:T(8,128)(2,1)}, u32[]{:S(2)}, u32[]{:S(2)}) collective-permute-start(bf16[8192,128]{1,0:T(8,128)(2,1)} %table_ref.1), channel_id=1, source_target_pairs={{0,1},{1,0},{2,3},{3,2},{4,5},{5,4},{6,7},{7,6},{8,9},{9,8},{10,11... | collective-permute-start | bytes 6291464 | tf_op jit(solution)/shard_map/ppermute | solution.py:178
  65.2 41.0 %copy-start.4 = (bf16[2864,128]{1,0:T(8,128)(2,1)}, bf16[2864,128]{1,0:T(8,128)(2,1)S(1)}, u32[]{:S(2)}) copy-start(bf16[2864,128]{1,0:T(8,128)(2,1)S(1)} %collective-permute-done.7) | copy-start | bytes 2199556
  65.2 19.1 %collective-permute-start.6 = (bf16[3280,128]{1,0:T(8,128)(2,1)S(1)}, bf16[3280,128]{1,0:T(8,128)(2,1)}, u32[]{:S(2)}, u32[]{:S(2)}) collective-permute-start(bf16[3280,128]{1,0:T(8,128)(2,1)S(1)} %get-tuple-element.16), channel_id=1, source_target_pairs={{0,24},{1,25},{2,26},{3,27},{4,28},{5,29},{6,30},{7,31},{8,0},{9,1... | collective-permute-start | bytes 2519048 | tf_op jit(solution)/shard_map/ppermute | solution.py:178
  66.1 40.1 %copy-start.5 = (bf16[2864,128]{1,0:T(8,128)(2,1)}, bf16[2864,128]{1,0:T(8,128)(2,1)S(1)}, u32[]{:S(2)}) copy-start(bf16[2864,128]{1,0:T(8,128)(2,1)S(1)} %collective-permute-done.8) | copy-start | bytes 2199556
  66.1 18.7 %collective-permute-start.15 = (bf16[2864,128]{1,0:T(8,128)(2,1)S(1)}, bf16[2864,128]{1,0:T(8,128)(2,1)S(1)}, u32[]{:S(2)}, u32[]{:S(2)}) collective-permute-start(bf16[2864,128]{1,0:T(8,128)(2,1)S(1)} %collective-permute-done.7), channel_id=1, source_target_pairs={{0,1},{1,0},{2,3},{3,2},{4,5},{5,4},{6,7},{7,6},{8,9},{9,8},{10,11... | collective-permute-start | bytes 2199560 | tf_op jit(solution)/shard_map/ppermute | solution.py:178
  67.6 17.4 %collective-permute-start.16 = (bf16[2864,128]{1,0:T(8,128)(2,1)S(1)}, bf16[2864,128]{1,0:T(8,128)(2,1)S(1)}, u32[]{:S(2)}, u32[]{:S(2)}) collective-permute-start(bf16[2864,128]{1,0:T(8,128)(2,1)S(1)} %collective-permute-done.8), channel_id=1, source_target_pairs={{0,1},{1,0},{2,3},{3,2},{4,5},{5,4},{6,7},{7,6},{8,9},{9,8},{10,11... | collective-permute-start | bytes 2199560 | tf_op jit(solution)/shard_map/ppermute | solution.py:178
  84.3 36.0 %collective-permute-start.12 = (bf16[4096,128]{1,0:T(8,128)(2,1)}, bf16[4096,128]{1,0:T(8,128)(2,1)}, u32[]{:S(2)}, u32[]{:S(2)}) collective-permute-start(bf16[4096,128]{1,0:T(8,128)(2,1)} %collective-permute-done.4), channel_id=1, source_target_pairs={{0,1},{1,0},{2,3},{3,2},{4,5},{5,4},{6,7},{7,6},{8,9},{9,8},{10,11... | collective-permute-start | bytes 3145736 | tf_op jit(solution)/shard_map/ppermute | solution.py:178
  84.3 21.9 %copy-start.3 = (bf16[4096,128]{1,0:T(8,128)(2,1)}, bf16[4096,128]{1,0:T(8,128)(2,1)S(1)}, u32[]{:S(2)}) copy-start(bf16[4096,128]{1,0:T(8,128)(2,1)S(1)} %collective-permute-done.10) | copy-start | bytes 3145732
  84.3 36.0 %collective-permute-start.11 = (bf16[4096,128]{1,0:T(8,128)(2,1)}, bf16[4096,128]{1,0:T(8,128)(2,1)}, u32[]{:S(2)}, u32[]{:S(2)}) collective-permute-start(bf16[4096,128]{1,0:T(8,128)(2,1)} %collective-permute-done.3), channel_id=1, source_target_pairs={{0,1},{1,0},{2,3},{3,2},{4,5},{5,4},{6,7},{7,6},{8,9},{9,8},{10,11... | collective-permute-start | bytes 3145736 | tf_op jit(solution)/shard_map/ppermute | solution.py:178
  84.8 35.5 %collective-permute-start.13 = (bf16[3280,128]{1,0:T(8,128)(2,1)}, bf16[3280,128]{1,0:T(8,128)(2,1)}, u32[]{:S(2)}, u32[]{:S(2)}) collective-permute-start(bf16[3280,128]{1,0:T(8,128)(2,1)} %collective-permute-done.5), channel_id=1, source_target_pairs={{0,1},{1,0},{2,3},{3,2},{4,5},{5,4},{6,7},{7,6},{8,9},{9,8},{10,11... | collective-permute-start | bytes 2519048 | tf_op jit(solution)/shard_map/ppermute | solution.py:178
  84.9 35.4 %collective-permute-start.14 = (bf16[3280,128]{1,0:T(8,128)(2,1)}, bf16[3280,128]{1,0:T(8,128)(2,1)}, u32[]{:S(2)}, u32[]{:S(2)}) collective-permute-start(bf16[3280,128]{1,0:T(8,128)(2,1)} %collective-permute-done.6), channel_id=1, source_target_pairs={{0,1},{1,0},{2,3},{3,2},{4,5},{5,4},{6,7},{7,6},{8,9},{9,8},{10,11... | collective-permute-start | bytes 2519048 | tf_op jit(solution)/shard_map/ppermute | solution.py:178
  106.2 14.1 %all-to-all-start.1 = ((s32[128,1,128]{2,1,0:T(1,128)}), s32[128,1,128]{2,1,0:T(1,128)S(1)}, u32[]{:S(2)}, u32[]{:S(2)}) async-start(s32[128,1,128]{2,1,0:T(1,128)} %bitcast.7), calls=%async_computation.1 | async-start | bytes 131072 | tf_op jit(solution)/shard_map/all_to_all | solution.py:275
  (2 other events, 42.7 us)

commit v6 on v5

--- a/solution.py
+++ b/solution.py
@@ -13,7 +13,7 @@
 BLOCKS = 32
 SHARD = 8192
 RING = (2, -1, 1)
-LARGE, SMALLER = (1248, 608, 608), (800, 416, 416)
+LARGE, SMALLER = (1216, 640, 640), (832, 448, 448)
 BOTH = tuple(large + smaller for large, smaller in zip(LARGE, SMALLER))
 REST = SHARD - 4 * BOTH[1]
 ENTRIES = 8 * SHARD
@@ -117,7 +117,8 @@
     pieces, out_ref, scratch = refs[:-11], refs[-11], refs[-10:]
     table_ref, pairs_ref, wide_ref, odd_ref, rows_ref, place_ref, scalar_ref, sem, place_sem, out_sem = scratch
     me = me_ref[0]
-    for piece, places in zip(pieces, table_parts(me, 0) + table_parts(me, 1)):
+    work = sorted(zip(pieces, table_parts(me, 0) + table_parts(me, 1)), key=lambda item: -item[0].shape[0] // len(item[1]))
+    for piece, places in work:
         at = 0
         for rows, base in places:
             pltpu.make_async_copy(
@@ -303,9 +304,7 @@
         compiler_params=SMALL,
         name="hold",
     )(me)
-    other_rest = []
-    for piece in rest:
-        other_rest.append(other_core(piece))
+    other_rest = [other_core(piece) for piece in rest]
     other_ring = [other_core(piece) for piece in ring[:2]]
     other_ring += [other_core(piece) for piece in ring[2:]]
     pieces = [decoding_table, every, *rest, *ring, other_table, other_every, *other_rest, *other_ring]

time: 134 us -> 137 us (1.022)
  waiting for transfers between devices: 75.9 us -> 78.4 us
    ppermute x17, waiting for transfers between devices: 67.9 us -> 70.3 us  [moved(): return lax.ppermute(x, ALL, pairs)]
  transfers between devices with their start and end apart: 18 -> 18, of which waited for: 6 -> 4; matrix products, arithmetic and copies ran while one was open for 1% -> 1% of each run, Pallas kernels for 2% -> 2%
where the time goes in v6:
time: 137 us; the launch traced here: 135 us
  waiting for transfers between devices  78.4 us (57%)
  starting transfers between devices  21.4 us (16%)
  blocking collectives  17.7 us (13%)
  Pallas kernels  15.5 us (11%)
  local copies, waits for them, and re-layouts  1.79 us (1%)
    ppermute x17, waiting for transfers between devices, moved(): return lax.ppermute(x, ALL, pairs)  70.3 us
    all_to_all x1, blocking collectives, exchange(): return lax.all_to_all(x, ALL, 0, 0, tiled=True)  17.7 us
    ppermute x17, starting transfers between devices, moved(): return lax.ppermute(x, ALL, pairs)  15.4 us
    pallas_call x1, Pallas kernels, steps(): pl.pallas_call(decode, out_shape=jax.ShapeDtypeStruct((BLOCKS * LANES, LA...  11.4 us
    all_to_all x1, waiting for transfers between devices, exchange(): return lax.all_to_all(x, ALL, 0, 0, tiled=True)  8.09 us
    all_to_all x1, starting transfers between devices, exchange(): return lax.all_to_all(x, ALL, 0, 0, tiled=True)  5.97 us
  transfers between devices with their start and end apart: 18, of which 4 were waited for; matrix products, arithmetic and copies ran while one was open for 1% of the time, Pallas kernels for 2%

profile of v6, /device:TPU:4, one launch (start us, length us, event | category | flops | bytes accessed | tf_op | source)
XLA Modules:
  0.0 134.8 jit_solution(6029250439884869077)
XLA Ops:
  0.0 1.2 cut.1
  1.2 4.0 %collective-permute-start = (bf16[2048,128]{1,0:T(8,128)(2,1)S(1)}, bf16[2048,128]{1,0:T(8,128)(2,1)S(1)}, u32[]{:S(2)}, u32[]{:S(2)}) collective-permute-start(bf16[2048,128]{1,0:T(8,128)(2,1)S(1)} %get-tuple-element.12), channel_id=1, source_target_pairs={{0,4},{1,5},{2,6},{3,7},{4,0},{5,1},{6,2},{7,3},{8,12},{9,13},{10,... | collective-permute-start | bytes 1572872 | tf_op jit(solution)/shard_map/ppermute | solution.py:179
  5.2 1.3 slice.3
  6.4 0.8 collective-permute-start.4
  7.2 1.3 collective-permute-start.3
  8.5 1.9 %collective-permute-start.2 = (bf16[1088,128]{1,0:T(8,128)(2,1)S(1)}, bf16[1088,128]{1,0:T(8,128)(2,1)S(1)}, u32[]{:S(2)}, u32[]{:S(2)}) collective-permute-start(bf16[1088,128]{1,0:T(8,128)(2,1)S(1)} %get-tuple-element.13), channel_id=1, source_target_pairs={{0,6},{1,7},{2,0},{3,1},{4,2},{5,3},{6,4},{7,5},{8,14},{9,15},{10,... | collective-permute-start | bytes 835592 | tf_op jit(solution)/shard_map/ppermute | solution.py:179
  10.6 34.3 %collective-permute-done.2.refs_2_ = bf16[1088,128]{1,0:T(8,128)(2,1)S(1)} collective-permute-done((bf16[1088,128]{1,0:T(8,128)(2,1)S(1)}, bf16[1088,128]{1,0:T(8,128)(2,1)S(1)}, u32[]{:S(2)}, u32[]{:S(2)}) %collective-permute-start.2) | collective-permute-done | bytes 278560 | tf_op jit(solution)/shard_map/ppermute | solution.py:179
  45.2 1.3 collective-permute-start.5
  46.5 1.6 %collective-permute-start.7 = (bf16[2976,128]{1,0:T(8,128)(2,1)S(1)}, bf16[2976,128]{1,0:T(8,128)(2,1)}, u32[]{:S(2)}, u32[]{:S(2)}) collective-permute-start(bf16[2976,128]{1,0:T(8,128)(2,1)S(1)} %get-tuple-element.17), channel_id=1, source_target_pairs={{0,32},{1,33},{2,34},{3,35},{4,36},{5,37},{6,38},{7,39},{8,40},{9,... | collective-permute-start | bytes 2285576 | tf_op jit(solution)/shard_map/ppermute | solution.py:179
  48.1 1.7 %collective-permute-start.8 = (bf16[2976,128]{1,0:T(8,128)(2,1)S(1)}, bf16[2976,128]{1,0:T(8,128)(2,1)}, u32[]{:S(2)}, u32[]{:S(2)}) collective-permute-start(bf16[2976,128]{1,0:T(8,128)(2,1)S(1)} %get-tuple-element.18), channel_id=1, source_target_pairs={{0,96},{1,97},{2,98},{3,99},{4,100},{5,101},{6,102},{7,103},{8,104... | collective-permute-start | bytes 2285576 | tf_op jit(solution)/shard_map/ppermute | solution.py:179
  49.8 0.5 collective-permute-start.10
  50.3 15.5 %collective-permute-done.7 = bf16[2976,128]{1,0:T(8,128)(2,1)} collective-permute-done((bf16[2976,128]{1,0:T(8,128)(2,1)S(1)}, bf16[2976,128]{1,0:T(8,128)(2,1)}, u32[]{:S(2)}, u32[]{:S(2)}) %collective-permute-start.7) | collective-permute-done | bytes 761888 | tf_op jit(solution)/shard_map/ppermute | solution.py:179
  65.8 0.5 collective-permute-start.11
  66.3 0.8 collective-permute-start.6
  67.1 20.4 %collective-permute-done.6 = bf16[3360,128]{1,0:T(8,128)(2,1)} collective-permute-done((bf16[3360,128]{1,0:T(8,128)(2,1)S(1)}, bf16[3360,128]{1,0:T(8,128)(2,1)}, u32[]{:S(2)}, u32[]{:S(2)}) %collective-permute-start.6) | collective-permute-done | bytes 860192 | tf_op jit(solution)/shard_map/ppermute | solution.py:179
  87.5 0.5 collective-permute-start.14
  88.1 0.4 collective-permute-start.16
  88.5 0.5 copy-done.6
  89.0 0.9 local_compaction.1
  90.0 17.7 %all_to_all.22 = s32[128,1,128]{2,1,0:T(1,128)S(1)} all-to-all(s32[128,1,128]{2,1,0:T(1,128)S(1)} %bitcast.30), channel_id=1, replica_groups=mesh['rows'=16,'dict'=8] {'rows','dict'}, dimensions={0} | all-to-all | bytes 131072 | tf_op jit(solution)/shard_map/all_to_all | solution.py:276
  107.6 1.7 %regroup.1 = s32[128,128]{1,0:T(8,128)} custom-call(s32[1]{0:T(128)} %bitcast.me_ref, s32[128,128]{1,0:T(8,128)S(1)} %bitcast.29), custom_call_target="tpu_custom_call" | custom-call | tf_op jit(solution)/shard_map/regroup/pallas_call | solution.py:290
  109.3 6.0 %all-to-all-start.1 = ((s32[128,1,128]{2,1,0:T(1,128)}), s32[128,1,128]{2,1,0:T(1,128)S(1)}, u32[]{:S(2)}, u32[]{:S(2)}) async-start(s32[128,1,128]{2,1,0:T(1,128)} %bitcast.7), calls=%async_computation.1 | async-start | bytes 131072 | tf_op jit(solution)/shard_map/all_to_all | solution.py:276
  115.3 8.1 %all-to-all-done.1 = s32[128,1,128]{2,1,0:T(1,128)S(1)} async-done(((s32[128,1,128]{2,1,0:T(1,128)}), s32[128,1,128]{2,1,0:T(1,128)S(1)}, u32[]{:S(2)}, u32[]{:S(2)}) %all-to-all-start.1) | async-done | bytes 65568 | tf_op jit(solution)/shard_map/all_to_all | solution.py:276
  123.4 11.4 %decode.1 = bf16[4096,128]{1,0:T(8,128)(2,1)} custom-call(s32[1]{0:T(128)} %bitcast.me_ref, s32[128,128]{1,0:T(8,128)S(1)} %bitcast.28, bf16[8192,128]{1,0:T(8,128)(2,1)S(1)} %hold.1.held_ref, bf16[4096,2,128]{2,1,0:T(2,128)(2,1)} %bitcast.9.refs_0_, bf16[2112,2,128]{2,1,0:T(2,128)(2,1)} %bitcast.27, bf16[1920,2,128]{2,1,0:T(2,128)(2,1)} %bitcast.35, ...), custom_call_target="tpu_custom_call" | custom-call | tf_op jit(solution)/shard_map/decode/pallas_call | solution.py:312
  (36 shorter events, 0.6 us)
Async XLA Ops:
  0.0 89.0 %copy-start.1 = (s32[4096]{0:T(1024)S(1)}, s32[4096]{0:T(1024)}, u32[]{:S(2)}) copy-start(s32[4096]{0:T(1024)} %param.3) | copy-start | bytes 49156
  0.0 89.0 %copy-start.2 = (s32[4096]{0:T(1024)S(1)}, s32[4096]{0:T(1024)}, u32[]{:S(2)}) copy-start(s32[4096]{0:T(1024)} %param.4) | copy-start | bytes 49156
  1.2 43.7 %collective-permute-start = (bf16[2048,128]{1,0:T(8,128)(2,1)S(1)}, bf16[2048,128]{1,0:T(8,128)(2,1)S(1)}, u32[]{:S(2)}, u32[]{:S(2)}) collective-permute-start(bf16[2048,128]{1,0:T(8,128)(2,1)S(1)} %get-tuple-element.12), channel_id=1, source_target_pairs={{0,4},{1,5},{2,6},{3,7},{4,0},{5,1},{6,2},{7,3},{8,12},{9,13},{10,... | collective-permute-start | bytes 1572872 | tf_op jit(solution)/shard_map/ppermute | solution.py:179
  6.4 43.3 %collective-permute-start.4 = (bf16[3840,128]{1,0:T(8,128)(2,1)S(1)}, bf16[3840,128]{1,0:T(8,128)(2,1)S(1)}, u32[]{:S(2)}, u32[]{:S(2)}) collective-permute-start(bf16[3840,128]{1,0:T(8,128)(2,1)S(1)} %slice.3), channel_id=1, source_target_pairs={{0,6},{1,7},{2,0},{3,1},{4,2},{5,3},{6,4},{7,5},{8,14},{9,15},{10,... | collective-permute-start | bytes 2949128 | tf_op jit(solution)/shard_map/ppermute | solution.py:179
  7.2 42.6 %collective-permute-start.3 = (bf16[3840,128]{1,0:T(8,128)(2,1)S(1)}, bf16[3840,128]{1,0:T(8,128)(2,1)S(1)}, u32[]{:S(2)}, u32[]{:S(2)}) collective-permute-start(bf16[3840,128]{1,0:T(8,128)(2,1)S(1)} %slice.3), channel_id=1, source_target_pairs={{0,2},{1,3},{2,4},{3,5},{4,6},{5,7},{6,0},{7,1},{8,10},{9,11},{10,... | collective-permute-start | bytes 2949128 | tf_op jit(solution)/shard_map/ppermute | solution.py:179
  8.5 36.4 %collective-permute-start.2 = (bf16[1088,128]{1,0:T(8,128)(2,1)S(1)}, bf16[1088,128]{1,0:T(8,128)(2,1)S(1)}, u32[]{:S(2)}, u32[]{:S(2)}) collective-permute-start(bf16[1088,128]{1,0:T(8,128)(2,1)S(1)} %get-tuple-element.13), channel_id=1, source_target_pairs={{0,6},{1,7},{2,0},{3,1},{4,2},{5,3},{6,4},{7,5},{8,14},{9,15},{10,... | collective-permute-start | bytes 835592 | tf_op jit(solution)/shard_map/ppermute | solution.py:179
  10.4 34.4 %collective-permute-start.1 = (bf16[1088,128]{1,0:T(8,128)(2,1)S(1)}, bf16[1088,128]{1,0:T(8,128)(2,1)S(1)}, u32[]{:S(2)}, u32[]{:S(2)}) collective-permute-start(bf16[1088,128]{1,0:T(8,128)(2,1)S(1)} %get-tuple-element.13), channel_id=1, source_target_pairs={{0,2},{1,3},{2,4},{3,5},{4,6},{5,7},{6,0},{7,1},{8,10},{9,11},{10,... | collective-permute-start | bytes 835592 | tf_op jit(solution)/shard_map/ppermute | solution.py:179
  45.2 78.2 %copy-start = (bf16[4224,128]{1,0:T(8,128)(2,1)}, bf16[4224,128]{1,0:T(8,128)(2,1)S(1)}, u32[]{:S(2)}) copy-start(bf16[4224,128]{1,0:T(8,128)(2,1)S(1)} %get-tuple-element.14) | copy-start | bytes 3244036
  45.2 21.0 %collective-permute-start.5 = (bf16[3360,128]{1,0:T(8,128)(2,1)S(1)}, bf16[3360,128]{1,0:T(8,128)(2,1)}, u32[]{:S(2)}, u32[]{:S(2)}) collective-permute-start(bf16[3360,128]{1,0:T(8,128)(2,1)S(1)} %get-tuple-element.15), channel_id=1, source_target_pairs={{0,8},{1,9},{2,10},{3,11},{4,12},{5,13},{6,14},{7,15},{8,16},{9,17... | collective-permute-start | bytes 2580488 | tf_op jit(solution)/shard_map/ppermute | solution.py:179
  46.5 19.3 %collective-permute-start.7 = (bf16[2976,128]{1,0:T(8,128)(2,1)S(1)}, bf16[2976,128]{1,0:T(8,128)(2,1)}, u32[]{:S(2)}, u32[]{:S(2)}) collective-permute-start(bf16[2976,128]{1,0:T(8,128)(2,1)S(1)} %get-tuple-element.17), channel_id=1, source_target_pairs={{0,32},{1,33},{2,34},{3,35},{4,36},{5,37},{6,38},{7,39},{8,40},{9,... | collective-permute-start | bytes 2285576 | tf_op jit(solution)/shard_map/ppermute | solution.py:179
  48.1 17.7 %collective-permute-start.8 = (bf16[2976,128]{1,0:T(8,128)(2,1)S(1)}, bf16[2976,128]{1,0:T(8,128)(2,1)}, u32[]{:S(2)}, u32[]{:S(2)}) collective-permute-start(bf16[2976,128]{1,0:T(8,128)(2,1)S(1)} %get-tuple-element.18), channel_id=1, source_target_pairs={{0,96},{1,97},{2,98},{3,99},{4,100},{5,101},{6,102},{7,103},{8,104... | collective-permute-start | bytes 2285576 | tf_op jit(solution)/shard_map/ppermute | solution.py:179
  49.8 59.5 %copy-start.4 = (bf16[3840,128]{1,0:T(8,128)(2,1)}, bf16[3840,128]{1,0:T(8,128)(2,1)S(1)}, u32[]{:S(2)}) copy-start(bf16[3840,128]{1,0:T(8,128)(2,1)S(1)} %collective-permute-done.4) | copy-start | bytes 2949124
  49.8 73.6 %collective-permute-start.9 = (bf16[8192,128]{1,0:T(8,128)(2,1)}, bf16[8192,128]{1,0:T(8,128)(2,1)}, u32[]{:S(2)}, u32[]{:S(2)}) collective-permute-start(bf16[8192,128]{1,0:T(8,128)(2,1)} %table_ref.1), channel_id=1, source_target_pairs={{0,1},{1,0},{2,3},{3,2},{4,5},{5,4},{6,7},{7,6},{8,9},{9,8},{10,11... | collective-permute-start | bytes 6291464 | tf_op jit(solution)/shard_map/ppermute | solution.py:179
  49.8 59.5 %copy-start.5 = (bf16[3840,128]{1,0:T(8,128)(2,1)}, bf16[3840,128]{1,0:T(8,128)(2,1)S(1)}, u32[]{:S(2)}) copy-start(bf16[3840,128]{1,0:T(8,128)(2,1)S(1)} %collective-permute-done.3) | copy-start | bytes 2949124
  49.8 37.7 %collective-permute-start.10 = (bf16[4224,128]{1,0:T(8,128)(2,1)S(1)}, bf16[4224,128]{1,0:T(8,128)(2,1)S(1)}, u32[]{:S(2)}, u32[]{:S(2)}) collective-permute-start(bf16[4224,128]{1,0:T(8,128)(2,1)S(1)} %get-tuple-element.14), channel_id=1, source_target_pairs={{0,1},{1,0},{2,3},{3,2},{4,5},{5,4},{6,7},{7,6},{8,9},{9,8},{10,11... | collective-permute-start | bytes 3244040 | tf_op jit(solution)/shard_map/ppermute | solution.py:179
  65.8 22.2 %collective-permute-start.12 = (bf16[3840,128]{1,0:T(8,128)(2,1)S(1)}, bf16[3840,128]{1,0:T(8,128)(2,1)S(1)}, u32[]{:S(2)}, u32[]{:S(2)}) collective-permute-start(bf16[3840,128]{1,0:T(8,128)(2,1)S(1)} %collective-permute-done.4), channel_id=1, source_target_pairs={{0,1},{1,0},{2,3},{3,2},{4,5},{5,4},{6,7},{7,6},{8,9},{9,8},{10,11... | collective-permute-start | bytes 2949128 | tf_op jit(solution)/shard_map/ppermute | solution.py:179
  65.8 22.3 %collective-permute-start.11 = (bf16[3840,128]{1,0:T(8,128)(2,1)S(1)}, bf16[3840,128]{1,0:T(8,128)(2,1)S(1)}, u32[]{:S(2)}, u32[]{:S(2)}) collective-permute-start(bf16[3840,128]{1,0:T(8,128)(2,1)S(1)} %collective-permute-done.3), channel_id=1, source_target_pairs={{0,1},{1,0},{2,3},{3,2},{4,5},{5,4},{6,7},{7,6},{8,9},{9,8},{10,11... | collective-permute-start | bytes 2949128 | tf_op jit(solution)/shard_map/ppermute | solution.py:179
  66.3 21.2 %collective-permute-start.6 = (bf16[3360,128]{1,0:T(8,128)(2,1)S(1)}, bf16[3360,128]{1,0:T(8,128)(2,1)}, u32[]{:S(2)}, u32[]{:S(2)}) collective-permute-start(bf16[3360,128]{1,0:T(8,128)(2,1)S(1)} %get-tuple-element.16), channel_id=1, source_target_pairs={{0,24},{1,25},{2,26},{3,27},{4,28},{5,29},{6,30},{7,31},{8,0},{9,1... | collective-permute-start | bytes 2580488 | tf_op jit(solution)/shard_map/ppermute | solution.py:179
  87.5 35.9 %collective-permute-start.13 = (bf16[3360,128]{1,0:T(8,128)(2,1)}, bf16[3360,128]{1,0:T(8,128)(2,1)}, u32[]{:S(2)}, u32[]{:S(2)}) collective-permute-start(bf16[3360,128]{1,0:T(8,128)(2,1)} %collective-permute-done.5), channel_id=1, source_target_pairs={{0,1},{1,0},{2,3},{3,2},{4,5},{5,4},{6,7},{7,6},{8,9},{9,8},{10,11... | collective-permute-start | bytes 2580488 | tf_op jit(solution)/shard_map/ppermute | solution.py:179
  87.5 35.9 %collective-permute-start.14 = (bf16[3360,128]{1,0:T(8,128)(2,1)}, bf16[3360,128]{1,0:T(8,128)(2,1)}, u32[]{:S(2)}, u32[]{:S(2)}) collective-permute-start(bf16[3360,128]{1,0:T(8,128)(2,1)} %collective-permute-done.6), channel_id=1, source_target_pairs={{0,1},{1,0},{2,3},{3,2},{4,5},{5,4},{6,7},{7,6},{8,9},{9,8},{10,11... | collective-permute-start | bytes 2580488 | tf_op jit(solution)/shard_map/ppermute | solution.py:179
  88.0 35.4 %collective-permute-start.15 = (bf16[2976,128]{1,0:T(8,128)(2,1)}, bf16[2976,128]{1,0:T(8,128)(2,1)}, u32[]{:S(2)}, u32[]{:S(2)}) collective-permute-start(bf16[2976,128]{1,0:T(8,128)(2,1)} %collective-permute-done.7), channel_id=1, source_target_pairs={{0,1},{1,0},{2,3},{3,2},{4,5},{5,4},{6,7},{7,6},{8,9},{9,8},{10,11... | collective-permute-start | bytes 2285576 | tf_op jit(solution)/shard_map/ppermute | solution.py:179
  88.1 21.2 %copy-start.7 = (bf16[3840,128]{1,0:T(8,128)(2,1)}, bf16[3840,128]{1,0:T(8,128)(2,1)S(1)}, u32[]{:S(2)}) copy-start(bf16[3840,128]{1,0:T(8,128)(2,1)S(1)} %collective-permute-done.11) | copy-start | bytes 2949124
  88.1 35.3 %collective-permute-start.16 = (bf16[2976,128]{1,0:T(8,128)(2,1)}, bf16[2976,128]{1,0:T(8,128)(2,1)}, u32[]{:S(2)}, u32[]{:S(2)}) collective-permute-start(bf16[2976,128]{1,0:T(8,128)(2,1)} %collective-permute-done.8), channel_id=1, source_target_pairs={{0,1},{1,0},{2,3},{3,2},{4,5},{5,4},{6,7},{7,6},{8,9},{9,8},{10,11... | collective-permute-start | bytes 2285576 | tf_op jit(solution)/shard_map/ppermute | solution.py:179
  109.3 14.1 %all-to-all-start.1 = ((s32[128,1,128]{2,1,0:T(1,128)}), s32[128,1,128]{2,1,0:T(1,128)S(1)}, u32[]{:S(2)}, u32[]{:S(2)}) async-start(s32[128,1,128]{2,1,0:T(1,128)} %bitcast.7), calls=%async_computation.1 | async-start | bytes 131072 | tf_op jit(solution)/shard_map/all_to_all | solution.py:276
  (2 other events, 2.1 us)
